TPU v7x, 32 devices: a whole 2x2x4 slice. The times are simulated.
32 devices in a mesh: dp: 2 (over x), ff: 4 (over z), hd: 4 (over y, core).
Axes of the slice: x: 2, y: 2, z: 4, core: 2. Of those that a mesh axis runs over, the one named last changes fastest.
Arguments:
- x_in: bfloat16 [256, 4096], P('dp', 'hd'), parts along dimension 0
- w_up: bfloat16 [4096, 20480], P('hd', 'ff')
- b_up: float32 [20480], P('ff')
- w_down: bfloat16 [10240, 4096], P('ff', 'hd')
- b_down: float32 [4096], P('hd')
- ln_gain: float32 [4096], P('hd')
- ln_bias: float32 [4096], P('hd')
- dy_in: bfloat16 [256, 4096], P('dp', 'hd'), parts along dimension 0
Outputs:
- output 1: bfloat16 [256, 4096], P('dp', 'hd'), parts along dimension 0
- output 2: bfloat16 [256, 4096], P('dp', 'hd'), parts along dimension 0
- output 3: float32 [8192, 20480], P(('dp', 'hd'), 'ff'), parts along dimension 0
- output 4: float32 [20480, 4096], P(('dp', 'ff'), 'hd'), parts along dimension 0
- output 5: float32 [40960], P(('dp', 'ff')), parts along dimension 0
- output 6: float32 [8192], P(('dp', 'hd')), parts along dimension 0
- output 7: float32 [8192], P(('dp', 'hd')), parts along dimension 0
- output 8: float32 [8192], P(('dp', 'hd')), parts along dimension 0
There are 2 independent parts. A program takes and returns all parts, laid end to end along the dimension named above; an argument that names none is the same for every part.
All inputs are finite; a program needn't handle non-finite values.
Results may differ from a plain program's by a relative error of at most 0.01878.
Values are sent between devices in bfloat16 or wider.
A program may use at most 1 GiB of HBM per device.

v0:
```python
import math
import jax
import jax.numpy as jnp
from jax import lax
from jax.sharding import PartitionSpec as P

PAIR = 128
ALPHA = math.sqrt(140.0)
LN_EPS = 1e-5


def gelu_tanh(z_val):
    return jax.nn.gelu(z_val, approximate=True)


def solution(mesh):
    hd_size = mesh.shape['hd']
    data_spec = P('dp', 'hd')
    hid_spec = P('hd')
    in_specs = (data_spec, P('hd', 'ff'), P('ff'), P('ff', 'hd'), hid_spec, hid_spec, hid_spec, data_spec)
    out_specs = (data_spec, data_spec, P(('dp', 'hd'), 'ff'), P(('dp', 'ff'), 'hd'), P(('dp', 'ff')), P(('dp', 'hd')), P(('dp', 'hd')), P(('dp', 'hd')))

    def device_step(x_loc, w_up, b_up, w_down, b_down, ln_gain, ln_bias, dy_loc):
        tokens, hid_loc = x_loc.shape
        hidden = hid_loc * hd_size
        n_blocks = w_up.shape[1] // (2 * PAIR)
        ffn_loc = n_blocks * PAIR
        w_up4 = w_up.reshape(hid_loc, n_blocks, 2, PAIR)
        u_part = jnp.einsum('th,hbkc->tbkc', x_loc, w_up4, preferred_element_type=jnp.float32)
        u_summed = lax.psum(u_part.astype(jnp.bfloat16), 'hd')
        u_act = (u_summed.astype(jnp.float32) + b_up.reshape(n_blocks, 2, PAIR)).astype(jnp.bfloat16)
        val_half = u_act[:, :, 0, :].astype(jnp.float32)
        gate_half = u_act[:, :, 1, :].astype(jnp.float32)
        gelu_out, gelu_vjp = jax.vjp(gelu_tanh, gate_half)
        m_act = (val_half * gelu_out).astype(jnp.bfloat16).reshape(tokens, ffn_loc)
        f_part = jnp.dot(m_act, w_down, preferred_element_type=jnp.float32)
        f_out = lax.psum(f_part.astype(jnp.bfloat16), 'ff').astype(jnp.float32)
        residual = ALPHA * x_loc.astype(jnp.float32) + f_out + b_down
        moments = lax.psum(jnp.stack([jnp.sum(residual, axis=1), jnp.sum(residual * residual, axis=1)]), 'hd')
        row_mean = (moments[0] / hidden)[:, None]
        inv_std = lax.rsqrt(moments[1][:, None] / hidden - row_mean * row_mean + LN_EPS)
        normed = (residual - row_mean) * inv_std
        y_loc = (ln_gain * normed + ln_bias).astype(jnp.bfloat16)
        dy_f = dy_loc.astype(jnp.float32)
        g_dy = dy_f * ln_gain
        grad_moments = lax.psum(jnp.stack([jnp.sum(g_dy, axis=1), jnp.sum(g_dy * normed, axis=1)]), 'hd')
        d_resid = inv_std * (g_dy - (grad_moments[0] / hidden)[:, None] - normed * (grad_moments[1] / hidden)[:, None])
        dr_b = d_resid.astype(jnp.bfloat16)
        dm_part = jnp.einsum('th,fh->tf', dr_b, w_down, preferred_element_type=jnp.float32)
        d_mact = lax.psum(dm_part.astype(jnp.bfloat16), 'hd').astype(jnp.float32).reshape(tokens, n_blocks, PAIR)
        dw_down = jnp.einsum('tf,th->fh', m_act, dr_b, preferred_element_type=jnp.float32)
        d_val = d_mact * gelu_out
        d_gate = gelu_vjp(d_mact * val_half)[0]
        du_f = jnp.stack([d_val, d_gate], axis=2)
        du_b = du_f.astype(jnp.bfloat16)
        dw_up = jnp.einsum('th,tbkc->hbkc', x_loc, du_b, preferred_element_type=jnp.float32).reshape(hid_loc, 2 * ffn_loc)
        dx_part = jnp.einsum('tbkc,hbkc->th', du_b, w_up4, preferred_element_type=jnp.float32)
        dx_sum = lax.psum(dx_part.astype(jnp.bfloat16), 'ff').astype(jnp.float32)
        dx_loc = (ALPHA * d_resid + dx_sum).astype(jnp.bfloat16)
        db_up = jnp.sum(du_f, axis=0).reshape(2 * ffn_loc)
        return (y_loc, dx_loc, dw_up, dw_down, db_up, jnp.sum(d_resid, axis=0), jnp.sum(dy_f * normed, axis=0), jnp.sum(dy_f, axis=0))

    return jax.shard_map(device_step, mesh=mesh, in_specs=in_specs, out_specs=out_specs, check_vma=False)
```

profile of v0, /device:TPU:0, one launch (start us, length us, event | category | flops | bytes accessed | tf_op | source)
XLA Modules:
  0.0 235.8 jit_solution(8340956737357122753)
XLA Ops:
  7.2 0.0 copy-start.1
  7.2 0.0 all-reduce.5.cloned.1.call-start
  7.2 23.3 %reshape.85 = bf16[1024,20,2,128]{3,2,1,0:T(2,128)(2,1)} reshape(bf16[1024,5120]{1,0:T(8,128)(2,1)} %param.9) | data formatting | bytes 20971520 | tf_op jit(solution)/shard_map/reshape | solution.py:28
  30.6 0.0 copy-done.1
  30.6 6.6 %fusion.6 = bf16[128,20,2,128]{3,0,2,1:T(8,128)(2,1)} fusion(bf16[1024,20,2,128]{3,2,1,0:T(2,128)(2,1)} %reshape.85, bf16[128,1024]{1,0:T(8,128)(2,1)S(1)} %copy-done.1), kind=kOutput, calls=%fused_computation.17 | convolution fusion | flops 1342832640 | bytes 12058624 | tf_op jit(solution)/shard_map/th,hbkc->tbkc/dot_general | solution.py:29
  37.2 0.0 copy-start.5
  37.2 0.0 all-reduce.5.cloned.1.call-update
  37.2 0.0 all-reduce.7.cloned.1.call-start
  37.2 42.1 %all-reduce.5.cloned.1.call-done = bf16[128,20,2,128]{3,0,2,1:T(8,128)(2,1)} async-done(((bf16[128,20,2,128]{3,0,2,1:T(8,128)(2,1)}), bf16[128,20,2,128]{3,0,2,1:T(8,128)(2,1)}) %all-reduce.5.cloned.1.call-update) | async-done | bytes 1310736 | tf_op jit(solution)/shard_map/psum | solution.py:30
  79.4 0.0 copy-done.5
  79.4 1.7 add_convert_fusion
  81.1 0.0 copy-start
  81.1 1.5 slice_convert_fusion
  82.6 0.0 copy-done
  82.6 0.4 copy.22
  83.0 1.7 copy.21
  84.7 0.5 fusion.24
  85.2 0.0 copy-start.4
  85.2 0.0 copy-start.3
  85.2 0.0 copy-start.6
  85.2 4.1 %convolution_convert_fusion.1 = bf16[128,1024]{1,0:T(8,128)(2,1)} fusion(bf16[128,2560]{0,1:T(8,128)(2,1)S(1)} %fusion.24, bf16[2560,1024]{1,0:T(8,128)(2,1)} %param.11), kind=kOutput, calls=%fused_computation.35 | convolution fusion | flops 671219712 | bytes 6160384 | tf_op jit(solution)/shard_map/dot_general | solution.py:36
  89.3 0.0 copy-start.7
  89.3 0.0 all-reduce.7.cloned.1.call-update
  89.3 0.0 all-reduce.9.cloned.1.call-start
  89.4 35.5 %all-reduce.7.cloned.1.call-done = bf16[128,1024]{1,0:T(8,128)(2,1)} async-done(((bf16[128,1024]{1,0:T(8,128)(2,1)}), bf16[128,1024]{1,0:T(8,128)(2,1)}) %all-reduce.7.cloned.1.call-update) | async-done | bytes 262160 | tf_op jit(solution)/shard_map/psum | solution.py:37
  124.9 0.0 copy-done.4
  124.9 0.0 copy-start.2
  124.9 1.2 fusion.38
  126.2 5.7 %psum.44 = f32[2,128]{1,0:T(2,128)S(1)} all-reduce(f32[2,128]{1,0:T(2,128)S(1)} %pad_maximum_fusion.1), channel_id=1, replica_groups=mesh['dp'=2,'ff'=4,'hd'=4] {'hd'}, use_global_device_ids=true, to_apply=%region_4.0 | all-reduce | flops 256 | bytes 2048 | tf_op jit(solution)/shard_map/psum | solution.py:39
  131.9 0.0 copy-done.3
  131.9 0.0 copy-done.6
  131.9 1.9 fusion.37
  133.8 6.6 %psum.45 = f32[2,128]{1,0:T(2,128)S(1)} all-reduce(f32[2,128]{1,0:T(2,128)S(1)} %pad_maximum_fusion.2), channel_id=1, replica_groups=mesh['dp'=2,'ff'=4,'hd'=4] {'hd'}, use_global_device_ids=true, to_apply=%region_7.0 | all-reduce | flops 256 | bytes 2048 | tf_op jit(solution)/shard_map/psum | solution.py:46
  140.4 0.0 copy-done.7
  140.4 0.0 copy-done.2
  140.4 1.6 fusion.51
  142.0 4.3 %convolution_convert_fusion = bf16[128,2560]{1,0:T(8,128)(2,1)S(1)} fusion(bf16[2560,1024]{1,0:T(8,128)(2,1)} %param.11, f32[128,1024]{1,0:T(8,128)S(1)} %get-tuple-element.31), kind=kOutput, calls=%fused_computation.4 | convolution fusion | flops 671547392 | bytes 6422528 | tf_op jit(solution)/shard_map/th,fh->tf/dot_general | solution.py:49
  146.3 0.3 copy.23
  146.7 1.1 copy.24
  147.8 0.0 all-reduce.9.cloned.1.call-update
  147.8 0.2 all-reduce.11.cloned.1.call-start
  148.0 5.6 %fusion.44 = f32[2560,1024]{1,0:T(8,128)} fusion(bf16[128,2560]{0,1:T(8,128)(2,1)S(1)} %fusion.24, f32[128,1024]{1,0:T(8,128)S(1)} %get-tuple-element.31), kind=kOutput, calls=%fused_computation.58 | convolution fusion | flops 671219712 | bytes 11665408 | tf_op jit(solution)/shard_map/tf,th->fh/dot_general | solution.py:51
  153.6 27.2 %all-reduce.9.cloned.1.call-done = bf16[128,20,1,128]{3,0,2,1:T(8,128)(2,1)} async-done(((bf16[128,20,1,128]{3,0,2,1:T(8,128)(2,1)}), bf16[128,20,1,128]{3,0,2,1:T(8,128)(2,1)}) %all-reduce.9.cloned.1.call-update) | async-done | bytes 655376 | tf_op jit(solution)/shard_map/psum | solution.py:50
  180.9 2.6 %convert_multiply_fusion.3 = (f32[128,20,1,128]{3,0,2,1:T(8,128)S(1)}, f32[128,20,1,128]{3,0,2,1:T(8,128)S(1)}) fusion(bf16[128,20,1,128]{3,0,2,1:T(8,128)(2,1)} %all-reduce.9.cloned.1.call-done, bf16[128,20,2,128]{3,0,2,1:T(8,128)(2,1)} %copy-done), kind=kLoop, calls=%fused_computation.16 | loop fusion | flops 8192000 | bytes 4587520 | tf_op jit(solution)/shard_map/mul | solution.py:52
  183.4 8.3 %fusion.28 = bf16[128,1024]{1,0:T(8,128)(2,1)} fusion(bf16[1024,20,2,128]{3,2,1,0:T(2,128)(2,1)} %reshape.85, f32[128,20,1,128]{3,0,2,1:T(8,128)S(1)} %get-tuple-element.33, f32[128,20,1,128]{3,0,2,1:T(8,128)S(1)} %get-tuple-element.32), kind=kOutput, calls=%fused_computation.36 | convolution fusion | flops 1342963712 | bytes 13369344 | tf_op jit(solution)/shard_map/tbkc,hbkc->th/dot_general | solution.py:57
  191.8 0.0 all-reduce.11.cloned.1.call-update
  191.8 8.6 %fusion.39 = f32[20,2,128,1024]{3,2,1,0:T(8,128)} fusion(bf16[128,1024]{1,0:T(8,128)(2,1)S(1)} %copy-done.1, f32[128,20,1,128]{3,0,2,1:T(8,128)S(1)} %get-tuple-element.33, f32[128,20,1,128]{3,0,2,1:T(8,128)S(1)} %get-tuple-element.32), kind=kOutput, calls=%fused_computation.55 | convolution fusion | flops 1342832640 | bytes 23855104 | tf_op jit(solution)/shard_map/th,tbkc->hbkc/dot_general | solution.py:56
  200.3 19.9 %copy.27 = f32[1024,5120]{1,0:T(8,128)} copy(f32[1024,5120]{0,1:T(8,128)} %bitcast.45) | data formatting | bytes 41943040
  220.2 0.8 fusion.4
  221.0 6.5 %all-reduce.11.cloned.1.call-done = bf16[128,1024]{1,0:T(8,128)(2,1)} async-done(((bf16[128,1024]{1,0:T(8,128)(2,1)}), bf16[128,1024]{1,0:T(8,128)(2,1)}) %all-reduce.11.cloned.1.call-update) | async-done | bytes 262160 | tf_op jit(solution)/shard_map/psum | solution.py:58
  227.5 1.7 add_convert_fusion.1
  (5 shorter events, 0.0 us)
Async XLA Ops:
  7.2 23.4 %copy-start.1 = (bf16[128,1024]{1,0:T(8,128)(2,1)S(1)}, bf16[128,1024]{1,0:T(8,128)(2,1)}, u32[]{:S(2)}) copy-start(bf16[128,1024]{1,0:T(8,128)(2,1)} %param.8) | copy-start | bytes 786436
  7.2 72.2 %all-reduce.5.cloned.1.call-start = ((), (), s32[]{:S(2)}) async-start(), calls=%async_computation | async-start | bytes 2621440 | tf_op jit(solution)/shard_map/psum | solution.py:30
  37.2 42.2 %copy-start.5 = (f32[5120]{0:T(1024)S(1)}, f32[5120]{0:T(1024)}, u32[]{:S(2)}) copy-start(f32[5120]{0:T(1024)} %param.10) | copy-start | bytes 61444
  37.2 87.7 %all-reduce.7.cloned.1.call-start = ((), (), s32[]{:S(2)}) async-start(), calls=%async_computation.1 | async-start | bytes 524288 | tf_op jit(solution)/shard_map/psum | solution.py:37
  81.1 1.5 copy-start
  85.2 39.8 %copy-start.4 = (f32[1024]{0:T(1024)S(1)}, f32[1024]{0:T(1024)}, u32[]{:S(2)}) copy-start(f32[1024]{0:T(1024)} %param.12) | copy-start | bytes 12292
  85.2 46.7 %copy-start.3 = (bf16[128,1024]{1,0:T(8,128)(2,1)S(1)}, bf16[128,1024]{1,0:T(8,128)(2,1)}, u32[]{:S(2)}) copy-start(bf16[128,1024]{1,0:T(8,128)(2,1)} %param.15) | copy-start | bytes 786436
  85.2 46.7 %copy-start.6 = (f32[1024]{0:T(1024)S(1)}, f32[1024]{0:T(1024)}, u32[]{:S(2)}) copy-start(f32[1024]{0:T(1024)} %param.13) | copy-start | bytes 12292
  89.3 51.1 %copy-start.7 = (f32[1024]{0:T(1024)S(1)}, f32[1024]{0:T(1024)}, u32[]{:S(2)}) copy-start(f32[1024]{0:T(1024)} %param.14) | copy-start | bytes 12292
  89.3 91.5 %all-reduce.9.cloned.1.call-start = ((), (), s32[]{:S(2)}) async-start(), calls=%async_computation.2 | async-start | bytes 1310720 | tf_op jit(solution)/shard_map/psum | solution.py:50
  124.9 15.5 %copy-start.2 = (bf16[128,1024]{1,0:T(8,128)(2,1)S(1)}, bf16[128,1024]{1,0:T(8,128)(2,1)}, u32[]{:S(2)}) copy-start(bf16[128,1024]{1,0:T(8,128)(2,1)} %all-reduce.7.cloned.1.call-done) | copy-start | bytes 786436
  147.8 79.7 %all-reduce.11.cloned.1.call-start = ((), (), s32[]{:S(2)}) async-start(), calls=%async_computation.3 | async-start | bytes 524288 | tf_op jit(solution)/shard_map/psum | solution.py:58
Sparse Core Ops, SparseCore 0:
  37.3 42.0 all-reduce.4
  89.5 35.4 all-reduce.6
  147.9 32.8 all-reduce.8
  191.9 35.5 all-reduce.10
where the time goes:
time: 237 us; the launch traced here: 236 us
  waiting for transfers between devices  111 us (47%)
  local copies, waits for them, and re-layouts  46.8 us (20%)
  matrix products  37.5 us (16%)
  between operations  13.9 us (6%)
  other arithmetic  13.5 us (6%)
  blocking collectives  12.3 us (5%)
    psum x1, waiting for transfers between devices, device_step(): u_summed = lax.psum(u_part.astype(jnp.bfloat16), 'hd')  42.1 us
    psum x1, waiting for transfers between devices, device_step(): f_out = lax.psum(f_part.astype(jnp.bfloat16), 'ff').astype(jnp.float32)  35.5 us
    psum x1, waiting for transfers between devices, device_step(): lax.psum(dm_part.astype(jnp.bfloat16), 'hd').astype(jnp.float32)  27.2 us
    reshape x1, local copies, waits for them, and re-layouts, device_step(): w_up4 = w_up.reshape(hid_loc, n_blocks, 2, PAIR)  23.3 us
    unnamed x17, local copies, waits for them, and re-layouts  19.9 us
    dot_general x1, matrix products, device_step(): jnp.einsum('th,tbkc->hbkc', x_loc, du_b, preferred_element_type=jnp.float32)  8.55 us
    dot_general x1, matrix products, device_step(): jnp.einsum('tbkc,hbkc->th', du_b, w_up4, preferred_element_type=jnp.float32)  8.32 us
    dot_general x1, matrix products, device_step(): jnp.einsum('th,hbkc->tbkc', x_loc, w_up4, preferred_element_type=jnp.floa...  6.61 us
  transfers between devices with their start and end apart: 4, of which 4 were waited for; matrix products, arithmetic and copies ran while one was open for 15% of the time, Pallas kernels for 0%

commit v1 on v0

v1 whole, which is shorter than its diff:
```python
import functools
import math

import jax
import jax.numpy as jnp
from jax import lax
from jax.experimental import pallas as pl
from jax.experimental.pallas import tpu as pltpu
from jax.sharding import PartitionSpec as P

PAIR = 128
ALPHA = math.sqrt(140.0)
LN_EPS = 1e-5
GELU_K = math.sqrt(2.0 / math.pi)
GELU_C = 0.044715
MESH = pl.DeviceIdType.MESH
F32 = jnp.float32
BF16 = jnp.bfloat16

GROUPS = 1
LOOKAHEAD = 3


def gelu_parts(z):
    t = jnp.tanh(GELU_K * (z + GELU_C * (z * z * z)))
    cdf = 0.5 * (1.0 + t)
    slope = cdf + z * (0.5 * (1.0 - t * t) * (GELU_K * (1.0 + (3.0 * GELU_C) * (z * z))))
    return z * cdf, slope


def dot_nt(a, b):
    return lax.dot_general(a, b, (((1,), (1,)), ((), ())), preferred_element_type=F32)


def dot_tn(a, b):
    return lax.dot_general(a, b, (((0,), (0,)), ((), ())), preferred_element_type=F32)


def main_kernel(
    x_ref, w1_hbm, b1_ref, w2_hbm, b2_ref, gam_ref, bet_ref, dy_ref,
    y_ref, m_ref, d_ref, du_ref, dx0_ref, dx1_ref, dx2_ref, dx3_ref, drz_ref, db1_ref, db2_ref, dgam_ref, dbet_ref,
    w1b, w2b, upart, uhalf, usend, uin, ubuf, mbuf, facc, zsend, zin, fsum, stat_in, tmp, dr_buf,
    npart, nhalf, nsend, nin, nbuf, dxacc,
    wsem, chunk_s, chunk_r, full_s, full_r, zsem_s, zsem_r, stat_s, stat_r,
):
    n_ch = w1b.shape[0]
    hid = x_ref.shape[1]
    tokens = x_ref.shape[0]
    hidden = 4 * hid
    tn = tokens // GROUPS
    rz = tn // 4
    cw = 8 * PAIR
    q = lax.axis_index('hd')
    z = lax.axis_index('ff')
    k = lax.rem(q, 2)
    y = lax.div(q, 2)
    pq = q + 1 - 2 * k
    yq = lax.rem(q + 2, 4)
    dq = lax.rem(pq + 2, 4)

    def remote(src, dst, ss, rs, **dev):
        return pltpu.make_async_remote_copy(src_ref=src, dst_ref=dst, send_sem=ss, recv_sem=rs, device_id=dev, device_id_type=MESH)

    w_copies = [pltpu.make_async_copy(w1_hbm.at[:, pl.ds(cw * c, cw)], w1b.at[c], wsem.at[c]) for c in range(n_ch)]
    w_copies += [pltpu.make_async_copy(w2_hbm.at[pl.ds(4 * PAIR * c, 4 * PAIR), :], w2b.at[c], wsem.at[n_ch + c]) for c in range(n_ch)]
    started = [0]

    def need_weight(i):
        while started[0] < min(i + LOOKAHEAD, 2 * n_ch):
            w_copies[started[0]].start()
            started[0] += 1

    need_weight(0)
    bar = pltpu.get_barrier_semaphore()
    for dz in range(4):
        for dh in range(4):
            if dz or dh:
                pl.semaphore_signal(bar, inc=1, device_id={'hd': lax.rem(q + dh, 4), 'ff': lax.rem(z + dz, 4)}, device_id_type=MESH)

    waits = []

    def make_group(g):
        row0 = g * tn
        rows = pl.ds(row0, tn)
        def ch(kind, c):
            return chunk_s.at[g, kind, c], chunk_r.at[g, kind, c]

        u_d2d = [remote(upart.at[g, c, 1 - k], uhalf.at[g, c], *ch(0, c), hd=pq) for c in range(n_ch)]
        u_y = [remote(usend.at[g, c], uin.at[g, c], *ch(1, c), hd=yq) for c in range(n_ch)]
        m_p = [remote(mbuf.at[g, c, q], mbuf.at[g, c, q], *ch(2, c), hd=pq) for c in range(n_ch)]
        m_y = [remote(mbuf.at[g, c, q], mbuf.at[g, c, q], *ch(3, c), hd=yq) for c in range(n_ch)]
        m_f = [remote(mbuf.at[g, c, yq], mbuf.at[g, c, yq], *ch(4, c), hd=pq) for c in range(n_ch)]
        n_d2d = [remote(npart.at[g, c, 1 - k], nhalf.at[g, c], *ch(5, c), hd=pq) for c in range(n_ch)]
        n_y = [remote(nsend.at[g, c], nin.at[g, c], *ch(6, c), hd=yq) for c in range(n_ch)]
        n_p = [remote(nbuf.at[g, c, q], nbuf.at[g, c, q], *ch(7, c), hd=pq) for c in range(n_ch)]
        n_yy = [remote(nbuf.at[g, c, q], nbuf.at[g, c, q], *ch(8, c), hd=yq) for c in range(n_ch)]
        n_f = [remote(nbuf.at[g, c, yq], nbuf.at[g, c, yq], *ch(9, c), hd=pq) for c in range(n_ch)]
        u_p = remote(ubuf.at[g, q], ubuf.at[g, q], full_s.at[g, 0], full_r.at[g, 0], hd=pq)
        u_yy = remote(ubuf.at[g, q], ubuf.at[g, q], full_s.at[g, 1], full_r.at[g, 1], hd=yq)
        u_f = remote(ubuf.at[g, yq], ubuf.at[g, yq], full_s.at[g, 2], full_r.at[g, 2], hd=pq)
        z_rs = [remote(zsend.at[g, lax.rem(z + d, 4)], zin.at[g, d - 1], zsem_s.at[g, 0, d - 1], zsem_r.at[g, 0, d - 1], ff=lax.rem(z + d, 4)) for d in range(1, 4)]
        z_ag = [remote(fsum.at[g, z], fsum.at[g, z], zsem_s.at[g, 1, d - 1], zsem_r.at[g, 1, d - 1], ff=lax.rem(z + d, 4)) for d in range(1, 4)]
        st = []
        for dz in range(4):
            for dh in range(4):
                if dz or dh:
                    i = dz * 4 + dh - 1
                    st.append(remote(stat_in.at[g, z, q], stat_in.at[g, z, q], stat_s.at[g, i], stat_r.at[g, i], hd=lax.rem(q + dh, 4), ff=lax.rem(z + dz, 4)))
        waits.extend(u_d2d + u_y + m_p + m_y + m_f + n_d2d + n_y + n_p + n_yy + n_f + [u_p, u_yy, u_f] + z_rs + z_ag + st)

        def s1(c):
            if g == 0:
                need_weight(c)
                w_copies[c].wait()
            for j in range(4):
                o = jnp.dot(x_ref[rows, :], w1b[c, :, 2 * PAIR * j:2 * PAIR * (j + 1)], preferred_element_type=F32)
                upart[g, c, j % 2, j // 2] = o.astype(BF16)
            if g == 0 and c == 0:
                pl.semaphore_wait(bar, 15)
            u_d2d[c].start()

        def s2(c):
            u_d2d[c].wait_recv()
            usend[g, c] = (upart[g, c, k, 1 - y].astype(F32) + uhalf[g, c, 1 - y].astype(F32)).astype(BF16)
            u_y[c].start()

        def s3(c):
            u_y[c].wait_recv()
            u = upart[g, c, k, y].astype(F32) + uhalf[g, c, y].astype(F32) + uin[g, c].astype(F32)
            u = (u + b1_ref[4 * c + q]).astype(BF16)
            ubuf[g, q, c] = u
            u = u.astype(F32)
            gl, _ = gelu_parts(u[:, PAIR:])
            mbuf[g, c, q] = (u[:, :PAIR] * gl).astype(BF16)
            m_y[c].start()
            m_p[c].start()

        def s4(c):
            m_y[c].wait_recv()
            m_f[c].start()

        def s5(c):
            if g == 0:
                need_weight(n_ch + c)
                w_copies[n_ch + c].wait()
            m_p[c].wait_recv()
            m_f[c].wait_recv()
            blocks = [mbuf[g, c, j] for j in range(4)]
            for j in range(4):
                m_ref[4 * c + j, rows, :] = blocks[j]
            m = jnp.concatenate(blocks, axis=1)
            for n in range(0, hid, 256):
                o = jnp.dot(m, w2b[c, :, n:n + 256], preferred_element_type=F32)
                if c:
                    facc[g, :, n:n + 256] += o
                else:
                    facc[g, :, n:n + 256] = o

        def u_gather():
            u_yy.start()
            u_p.start()

        def u_forward():
            u_yy.wait_recv()
            u_f.start()

        def u_done():
            u_p.wait_recv()
            u_f.wait_recv()

        def z1():
            for b in range(4):
                zsend[g, b] = facc[g, b * rz:(b + 1) * rz, :].astype(BF16)
            for d in (2, 1, 3):
                z_rs[d - 1].start()

        def z2():
            off = pl.multiple_of(z * rz, rz)
            f = facc[g, pl.ds(off, rz), :]
            for d in (1, 3, 2):
                z_rs[d - 1].wait_recv()
                f = f + zin[g, d - 1].astype(F32)
            f = f.astype(BF16)
            fsum[g, z] = f
            for d in (2, 1, 3):
                z_ag[d - 1].start()
            xoff = pl.multiple_of(row0 + z * rz, rz)
            r = ALPHA * x_ref[pl.ds(xoff, rz), :].astype(F32) + f.astype(F32) + b2_ref[...]
            gd = dy_ref[pl.ds(xoff, rz), :].astype(F32) * gam_ref[...]
            mean = jnp.sum(r, axis=1, keepdims=True) * (1.0 / hid)
            cen = r - mean
            m2 = jnp.sum(cen * cen, axis=1, keepdims=True)
            sg = jnp.sum(gd, axis=1, keepdims=True)
            sgr = jnp.sum(gd * cen, axis=1, keepdims=True)
            lane = lax.broadcasted_iota(jnp.int32, (rz, 128), 1)
            vals = jnp.where(lane == 0, mean, jnp.where(lane == 1, m2, jnp.where(lane == 2, sg, jnp.where(lane == 3, sgr, 0.0))))
            tmp[...] = jnp.zeros_like(tmp)
            tmp[pl.ds(off, rz), :] = vals
            stat_in[g, z, q] = tmp[...].T[:8, :]
            for s in st:
                s.start()

        def z3():
            for s in st:
                s.wait_recv()
            per = [sum(stat_in[g, a, h] for a in range(4)) for h in range(4)]
            mu = sum(p[0:1, :] for p in per) * 0.25
            m2 = sum(p[1:2, :] + float(hid) * (p[0:1, :] - mu) * (p[0:1, :] - mu) for p in per)
            rho = lax.rsqrt(m2 * (1.0 / hidden) + LN_EPS)
            mg = sum(p[2:3, :] for p in per) * (1.0 / hidden)
            mgr = rho * sum(p[3:4, :] + (p[0:1, :] - mu) * p[2:3, :] for p in per) * (1.0 / hidden)
            tmp[0:1, :] = mu
            tmp[1:2, :] = rho
            tmp[2:3, :] = mg
            tmp[3:4, :] = mgr
            cols = tmp[...].T
            tmp[...] = cols
            for d in range(3):
                z_ag[d].wait_recv()
            for b in range(4):
                rr = pl.ds(row0 + b * rz, rz)
                c4 = tmp[b * rz:(b + 1) * rz, :]
                r = ALPHA * x_ref[rr, :].astype(F32) + fsum[g, b].astype(F32) + b2_ref[...]
                dy = dy_ref[rr, :].astype(F32)
                rhat = (r - c4[:, 0:1]) * c4[:, 1:2]
                y_ref[rr, :] = (gam_ref[...] * rhat + bet_ref[...]).astype(BF16)
                dr = c4[:, 1:2] * (dy * gam_ref[...] - c4[:, 2:3] - rhat * c4[:, 3:4])
                dr_buf[rr, :] = dr
                d_ref[rr, :] = dr.astype(BF16)
                sums = (jnp.sum(dr, axis=0, keepdims=True), jnp.sum(dy * rhat, axis=0, keepdims=True), jnp.sum(dy, axis=0, keepdims=True))
                for out, s in zip((db2_ref, dgam_ref, dbet_ref), sums):
                    if g == 0 and b == 0:
                        out[...] = s
                    else:
                        out[...] += s

        def t1(c):
            for h in range(2):
                o = dot_nt(d_ref[rows, :], w2b[c, 256 * h:256 * (h + 1), :]).astype(BF16)
                npart[g, c, 0, h] = o[:, :PAIR]
                npart[g, c, 1, h] = o[:, PAIR:]
            n_d2d[c].start()

        def t2(c):
            n_d2d[c].wait_recv()
            nsend[g, c] = (npart[g, c, k, 1 - y].astype(F32) + nhalf[g, c, 1 - y].astype(F32)).astype(BF16)
            n_y[c].start()

        def t3(c):
            n_y[c].wait_recv()
            nbuf[g, c, q] = (npart[g, c, k, y].astype(F32) + nhalf[g, c, y].astype(F32) + nin[g, c].astype(F32)).astype(BF16)
            n_yy[c].start()
            n_p[c].start()

        def t4(c):
            n_yy[c].wait_recv()
            n_f[c].start()

        def t5(c):
            n_p[c].wait_recv()
            n_f[c].wait_recv()
            parts = []
            for j in range(4):
                dm = nbuf[g, c, j].astype(F32)
                u = ubuf[g, j, c].astype(F32)
                gl, slope = gelu_parts(u[:, PAIR:])
                dv = dm * gl
                dg = dm * u[:, :PAIR] * slope
                duf = jnp.concatenate([dv, dg], axis=1)
                s = jnp.sum(duf, axis=0, keepdims=True)
                if g == 0:
                    db1_ref[4 * c + j] = s
                else:
                    db1_ref[4 * c + j] += s
                du = duf.astype(BF16)
                du_ref[4 * c + j, rows, :] = du
                parts.append(du)
            du = jnp.concatenate(parts, axis=1)
            for n in range(0, hid, 256):
                o = dot_nt(du, w1b[c, n:n + 256, :])
                if c:
                    dxacc[rows, n:n + 256] += o
                else:
                    dxacc[rows, n:n + 256] = o

        fwd = [functools.partial(s1, 0)]
        for c in range(1, n_ch):
            fwd += [functools.partial(s1, c), functools.partial(s2, c - 1)]
        fwd += [functools.partial(s2, n_ch - 1), functools.partial(s3, 0)]
        for c in range(1, n_ch):
            fwd += [functools.partial(s3, c), functools.partial(s4, c - 1)]
            if c > 1:
                fwd += [functools.partial(s5, c - 2)]
        fwd += [u_gather, functools.partial(s5, n_ch - 2), functools.partial(s4, n_ch - 1), functools.partial(s5, n_ch - 1)]
        mid = [z1, z2, u_forward, z3]
        bwd = [functools.partial(t1, 0)]
        for c in range(1, n_ch):
            bwd += [functools.partial(t1, c), functools.partial(t2, c - 1)]
        bwd += [functools.partial(t2, n_ch - 1), u_done, functools.partial(t3, 0)]
        for c in range(1, n_ch):
            bwd += [functools.partial(t3, c), functools.partial(t4, c - 1)]
            if c > 1:
                bwd += [functools.partial(t5, c - 2)]
        bwd += [functools.partial(t5, n_ch - 2), functools.partial(t4, n_ch - 1), functools.partial(t5, n_ch - 1)]
        return fwd, mid, bwd

    groups = [make_group(g) for g in range(GROUPS)]
    for part in range(3):
        for fwd_mid_bwd in groups:
            for step in fwd_mid_bwd[part]:
                step()

    rt = tokens // 4
    for d, out in enumerate((dx0_ref, dx1_ref, dx2_ref, dx3_ref)):
        off = pl.multiple_of(lax.rem(z + d, 4) * rt, rt)
        o = dxacc[pl.ds(off, rt), :]
        if d == 0:
            drz_ref[...] = ALPHA * dr_buf[pl.ds(off, rt), :] + o
            out[...] = o.astype(BF16)
        else:
            out[...] = o.astype(BF16)
    for w in waits:
        w.wait_send()


def dw2_kernel(m_ref, d_ref, o_ref):
    for j in range(m_ref.shape[0]):
        o_ref[PAIR * j:PAIR * (j + 1), :] = dot_tn(m_ref[j], d_ref[...])


def dw1_kernel(x_ref, du_ref, y_in, db1_in, db2_in, dg_in, dbt_in, o_ref, y_ref, db1_ref, db2_ref, dg_ref, dbt_ref):
    for j in range(du_ref.shape[0]):
        o_ref[:, 2 * PAIR * j:2 * PAIR * (j + 1)] = dot_tn(x_ref[...], du_ref[j])

    @pl.when(pl.program_id(0) == 0)
    def _():
        y_ref[...] = y_in[...]
        db1_ref[...] = db1_in[...]
        db2_ref[...] = db2_in[...]
        dg_ref[...] = dg_in[...]
        dbt_ref[...] = dbt_in[...]


def place_kernel(a_ref, b_ref, c_ref, d_ref, o_ref):
    z = lax.axis_index('ff')
    rt = a_ref.shape[0]
    for d, ref in enumerate((a_ref, b_ref, c_ref, d_ref)):
        o_ref[pl.ds(pl.multiple_of(lax.rem(z + 4 - d, 4) * rt, rt), rt), :] = ref[...]


def solution(mesh):
    data_spec = P('dp', 'hd')
    hid_spec = P('hd')
    in_specs = (data_spec, P('hd', 'ff'), P('ff'), P('ff', 'hd'), hid_spec, hid_spec, hid_spec, data_spec)
    out_specs = (data_spec, data_spec, P(('dp', 'hd'), 'ff'), P(('dp', 'ff'), 'hd'), P(('dp', 'ff')), P(('dp', 'hd')), P(('dp', 'hd')), P(('dp', 'hd')))
    n_ff = mesh.shape['ff']
    vmem = pl.BlockSpec(memory_space=pltpu.VMEM)
    hbm = pl.BlockSpec(memory_space=pl.ANY)
    S = jax.ShapeDtypeStruct

    def device_step(x_loc, w_up, b_up, w_down, b_down, ln_gain, ln_bias, dy_loc):
        tokens, hid = x_loc.shape
        n_blocks = w_up.shape[1] // (2 * PAIR)
        n_ch = n_blocks // 4
        tn = tokens // GROUPS
        rt = tokens // 4
        g = GROUPS
        dma = pltpu.SemaphoreType.DMA
        outs = pl.pallas_call(
            main_kernel,
            out_shape=(
                S((tokens, hid), BF16), S((n_blocks, tokens, PAIR), BF16), S((tokens, hid), BF16), S((n_blocks, tokens, 2 * PAIR), BF16),
                S((rt, hid), BF16), S((rt, hid), BF16), S((rt, hid), BF16), S((rt, hid), BF16), S((rt, hid), F32),
                S((n_blocks, 1, 2 * PAIR), F32), S((1, hid), F32), S((1, hid), F32), S((1, hid), F32),
            ),
            in_specs=[vmem, hbm, vmem, hbm, vmem, vmem, vmem, vmem],
            out_specs=[vmem] * 13,
            scratch_shapes=[
                pltpu.VMEM((n_ch, hid, 8 * PAIR), BF16), pltpu.VMEM((n_ch, 4 * PAIR, hid), BF16),
                pltpu.VMEM((g, n_ch, 2, 2, tn, 2 * PAIR), BF16), pltpu.VMEM((g, n_ch, 2, tn, 2 * PAIR), BF16),
                pltpu.VMEM((g, n_ch, tn, 2 * PAIR), BF16), pltpu.VMEM((g, n_ch, tn, 2 * PAIR), BF16),
                pltpu.VMEM((g, 4, n_ch, tn, 2 * PAIR), BF16), pltpu.VMEM((g, n_ch, 4, tn, PAIR), BF16),
                pltpu.VMEM((g, tn, hid), F32), pltpu.VMEM((g, 4, tn // 4, hid), BF16), pltpu.VMEM((g, 3, tn // 4, hid), BF16),
                pltpu.VMEM((g, 4, tn // 4, hid), BF16), pltpu.VMEM((g, 4, 4, 8, 128), F32), pltpu.VMEM((128, 128), F32),
                pltpu.VMEM((tokens, hid), F32),
                pltpu.VMEM((g, n_ch, 2, 2, tn, PAIR), BF16), pltpu.VMEM((g, n_ch, 2, tn, PAIR), BF16),
                pltpu.VMEM((g, n_ch, tn, PAIR), BF16), pltpu.VMEM((g, n_ch, tn, PAIR), BF16),
                pltpu.VMEM((g, n_ch, 4, tn, PAIR), BF16), pltpu.VMEM((tokens, hid), F32),
                dma((2 * n_ch,)), dma((g, 10, n_ch)), dma((g, 10, n_ch)), dma((g, 3)), dma((g, 3)),
                dma((g, 2, 3)), dma((g, 2, 3)), dma((g, 15)), dma((g, 15)),
            ],
            compiler_params=pltpu.CompilerParams(collective_id=0, has_side_effects=True, vmem_limit_bytes=48 * 2**20),
            name='mlp_main',
        )(x_loc, w_up, b_up.reshape(n_blocks, 1, 2 * PAIR), w_down, b_down.reshape(1, hid), ln_gain.reshape(1, hid), ln_bias.reshape(1, hid), dy_loc)
        y_a, m_a, d_a, du_a, _, dx1, dx2, dx3, drz, db1, db2, dgam, dbet = outs

        def shift(v, d):
            return lax.ppermute(v, 'ff', [(i, (i + d) % n_ff) for i in range(n_ff)])

        parts = [shift(v, d + 1) for d, v in enumerate((dx1, dx2, dx3))]
        mb = 2
        dw_down = pl.pallas_call(
            dw2_kernel,
            grid=(n_blocks // mb,),
            out_shape=S((n_blocks * PAIR, hid), F32),
            in_specs=[pl.BlockSpec((mb, tokens, PAIR), lambda i: (i, 0, 0)), vmem],
            out_specs=pl.BlockSpec((mb * PAIR, hid), lambda i: (i, 0)),
            cost_estimate=pl.CostEstimate(flops=2 * tokens * n_blocks * PAIR * hid * 3, bytes_accessed=4 * n_blocks * PAIR * hid, transcendentals=0),
            name='mlp_dw2',
        )(m_a, d_a)
        own = (drz + sum(p.astype(F32) for p in parts)).astype(BF16)
        back = [shift(own, d) for d in (1, 2, 3)]
        hb = PAIR
        dw_up, y_o, db1_o, db2_o, dg_o, dbt_o = pl.pallas_call(
            dw1_kernel,
            grid=(hid // hb,),
            out_shape=(S((hid, n_blocks * 2 * PAIR), F32), S(y_a.shape, BF16), S(db1.shape, F32), S(db2.shape, F32), S(db2.shape, F32), S(db2.shape, F32)),
            in_specs=[pl.BlockSpec((tokens, hb), lambda i: (0, i)), vmem, vmem, vmem, vmem, vmem, vmem],
            out_specs=[pl.BlockSpec((hb, n_blocks * 2 * PAIR), lambda i: (i, 0)), vmem, vmem, vmem, vmem, vmem],
            cost_estimate=pl.CostEstimate(flops=2 * tokens * n_blocks * 2 * PAIR * hid * 3, bytes_accessed=8 * n_blocks * PAIR * hid, transcendentals=0),
            name='mlp_dw1',
        )(x_loc, du_a, y_a, db1, db2, dgam, dbet)
        dx = pl.pallas_call(
            place_kernel,
            out_shape=S((tokens, hid), BF16),
            in_specs=[vmem] * 4,
            out_specs=vmem,
            name='mlp_place',
        )(own, *back)
        return (y_o, dx, dw_up, dw_down, db1_o.reshape(-1), db2_o.reshape(-1), dg_o.reshape(-1), dbt_o.reshape(-1))

    return jax.shard_map(device_step, mesh=mesh, in_specs=in_specs, out_specs=out_specs, check_vma=False)
```

time: 237 us -> 102 us (0.43)
  waiting for transfers between devices: 111 us -> 0.02 us
  Pallas kernels: 0 us -> 80.1 us
  matrix products: 37.5 us -> 0 us
  local copies, waits for them, and re-layouts: 46.8 us -> 11 us
  other arithmetic: 13.5 us -> 0.03 us
  between operations: 13.9 us -> 0.75 us
  blocking collectives: 12.3 us -> 0 us
  starting transfers between devices: 0.34 us -> 8.83 us
    psum x4 -> x0, waiting for transfers between devices: 111 us -> none  [the longest x1 42.1 us: device_step(): u_summed = lax.psum(u_part.astype(jnp.bfloat16), 'hd')]
    pallas_call x0 -> x4, Pallas kernels: none -> 80.1 us  [the longest x1 59.3 us: device_step(): pl.pallas_call(main_kernel, out_shape=(S((tokens, hid), BF16), S((n_block...]
    dot_general x6 -> x0, matrix products: 37.5 us -> none  [the longest x1 8.55 us: device_step(): jnp.einsum('th,tbkc->hbkc', x_loc, du_b, preferred_element_type=jnp.float32)]
    reshape x2 -> x0, local copies, waits for them, and re-layouts: 24.4 us -> none  [the longest x1 23.3 us: device_step(): w_up4 = w_up.reshape(hid_loc, n_blocks, 2, PAIR)]
    psum x2 -> x0, blocking collectives: 12.3 us -> none  [the longest x1 6.61 us: device_step(): lax.psum(jnp.stack([jnp.sum(g_dy, axis=1), jnp.sum(g_dy * normed, axis=1)...]
    unnamed x17 -> x36, local copies, waits for them, and re-layouts: 19.9 us -> 11 us
    ppermute x0 -> x6, starting transfers between devices: none -> 8.83 us  [shift(): return lax.ppermute(v, 'ff', [(i, (i + d) % n_ff) for i in range(n_ff)])]
    reduce_sum x4 -> x0, other arithmetic: 5.54 us -> none  [the longest x1 1.91 us: device_step(): jnp.sum(dy_f * normed, axis=0)]
  transfers between devices with their start and end apart: 4 -> 6, of which waited for: 4 -> 0; matrix products, arithmetic and copies ran while one was open for 15% -> 0% of each run, Pallas kernels for 0% -> 19%
where the time goes in v1:
time: 102 us; the launch traced here: 101 us
  Pallas kernels  80.1 us (79%)
  local copies, waits for them, and re-layouts  11 us (11%)
  starting transfers between devices  8.83 us (9%)
    pallas_call x1, Pallas kernels, device_step(): pl.pallas_call(main_kernel, out_shape=(S((tokens, hid), BF16), S((n_block...  59.3 us
    unnamed x36, local copies, waits for them, and re-layouts  11 us
    pallas_call x1, Pallas kernels, device_step(): pl.pallas_call(dw1_kernel, grid=(hid // hb,), out_shape=(S((hid, n_blocks...  10.4 us
    ppermute x6, starting transfers between devices, shift(): return lax.ppermute(v, 'ff', [(i, (i + d) % n_ff) for i in range(n_ff)])  8.83 us
    pallas_call x1, Pallas kernels, device_step(): pl.pallas_call(dw2_kernel, grid=(n_blocks // mb,), out_shape=S((n_blocks...  8.67 us
  transfers between devices with their start and end apart: 6, of which 0 were waited for; matrix products, arithmetic and copies ran while one was open for 0% of the time, Pallas kernels for 19%

profile of v1, /device:TPU:0, one launch (start us, length us, event | category | flops | bytes accessed | tf_op | source)
XLA Modules:
  0.0 100.8 jit_solution(13673353659094137723)
XLA Ops:
  0.6 0.0 copy-start.1
  0.6 0.9 copy-done.1
  1.6 0.0 copy-start.2
  1.6 0.9 copy-done.2
  2.5 0.0 copy-start.4
  2.5 0.7 copy-done.4
  3.3 0.0 copy-start.5
  3.3 0.7 copy-done.5
  4.0 0.0 copy-start.6
  4.0 0.7 copy-done.6
  4.6 0.0 copy-start.7
  4.6 0.7 copy-done.7
  5.3 59.3 %mlp_main.1 = (bf16[128,1024]{1,0:T(8,128)(2,1)S(1)}, bf16[20,128,128]{2,1,0:T(8,128)(2,1)S(1)}, bf16[128,1024]{1,0:T(8,128)(2,1)S(1)}, bf16[20,128,256]{2,1,0:T...) custom-call(bf16[128,1024]{1,0:T(8,128)(2,1)S(1)} %copy-done.2, ...), custom_call_target="tpu_custom_call" | custom-call | tf_op jit(solution)/shard_map/mlp_main/pallas_call | solution.py:369
  64.7 0.0 copy-start
  64.7 0.8 copy-done
  65.5 0.0 copy-start.3
  65.5 0.7 copy-done.3
  66.3 0.0 copy-start.8
  66.3 1.1 %copy-done.8 = bf16[20,128,256]{2,1,0:T(8,128)(2,1)} copy-done((bf16[20,128,256]{2,1,0:T(8,128)(2,1)}, bf16[20,128,256]{2,1,0:T(8,128)(2,1)S(1)}, u32[]{:S(2)}) %copy-start.8) | copy-done | bytes 1310744
  67.3 0.0 copy-start.9
  67.3 0.7 copy-done.9
  68.0 0.0 copy-start.10
  68.0 0.6 copy-done.10
  68.6 0.0 copy-start.12
  68.6 0.6 copy-done.12
  69.2 0.0 copy-start.13
  69.2 0.6 copy-done.13
  69.8 0.0 copy-start.11
  69.8 0.7 collective-permute-start
  70.5 2.2 %collective-permute-start.1 = (bf16[32,1024]{1,0:T(8,128)(2,1)S(1)}, bf16[32,1024]{1,0:T(8,128)(2,1)S(1)}, u32[]{:S(2)}, u32[]{:S(2)}) collective-permute-start(bf16[32,1024]{1,0:T(8,128)(2,1)S(1)} %get-tuple-element.35), channel_id=1, source_target_pairs={{0,8},{4,12},{8,0},{12,4},{1,9},{5,13},{9,1},{13,5},{2,10},{6,14},... | collective-permute-start | bytes 196616 | tf_op jit(solution)/shard_map/ppermute | solution.py:398
  72.8 1.1 %collective-permute-start.2 = (bf16[32,1024]{1,0:T(8,128)(2,1)S(1)}, bf16[32,1024]{1,0:T(8,128)(2,1)S(1)}, u32[]{:S(2)}, u32[]{:S(2)}) collective-permute-start(bf16[32,1024]{1,0:T(8,128)(2,1)S(1)} %get-tuple-element.36), channel_id=1, source_target_pairs={{0,12},{4,0},{8,4},{12,8},{1,13},{5,1},{9,5},{13,9},{2,14},{6,2},{... | collective-permute-start | bytes 196616 | tf_op jit(solution)/shard_map/ppermute | solution.py:398
  73.9 0.0 copy-done.11
  73.9 10.4 %mlp_dw1.1 = (f32[1024,5120]{1,0:T(8,128)}, bf16[128,1024]{1,0:T(8,128)(2,1)}, f32[20,1,256]{2,1,0:T(1,128)}, f32[1,1024]{1,0:T(1,128)}, f32[1,1024]{1,0:T(1,128)}, /*index=5*/f32[1,1024]{1,0:T(1,128)}) custom-call(bf16[128,1024]{1,0:T(8,128)(2,1)} %x_ref.3, bf16[20,128,256]{2,1,0:T(8,128)(2,1)} %copy-done.8, bf16[128,1024]{1,0:T(8,128)(2,1)} %copy-done.9, ...), custom_call_target="tpu_custom_call" | custom-call | flops 4026531840 | bytes 20971520 | tf_op jit(solution)/shard_map/mlp_dw1/pallas_call | solution.py:414
  84.3 0.0 collective-permute-done
  84.3 0.0 collective-permute-done.1
  84.3 0.0 collective-permute-done.2
  84.4 0.0 copy-start.14
  84.4 1.0 collective-permute-start.3
  85.4 1.0 collective-permute-start.4
  86.3 2.8 %collective-permute-start.5 = (bf16[32,1024]{1,0:T(8,128)(2,1)S(1)}, bf16[32,1024]{1,0:T(8,128)(2,1)S(1)}, u32[]{:S(2)}, u32[]{:S(2)}) collective-permute-start(bf16[32,1024]{1,0:T(8,128)(2,1)S(1)} %add_convert_fusion.a_ref), channel_id=1, source_target_pairs={{0,12},{4,0},{8,4},{12,8},{1,13},{5,1},{9,5},{13,9},{2,14},{6,2},{... | collective-permute-start | bytes 196616 | tf_op jit(solution)/shard_map/ppermute | solution.py:398
  89.2 8.7 %mlp_dw2.1 = f32[2560,1024]{1,0:T(8,128)} custom-call(bf16[20,128,128]{2,1,0:T(8,128)(2,1)} %copy-done, bf16[128,1024]{1,0:T(8,128)(2,1)} %copy-done.3), custom_call_target="tpu_custom_call" | custom-call | flops 2013265920 | bytes 10485760 | tf_op jit(solution)/shard_map/mlp_dw2/pallas_call | solution.py:402
  97.8 0.0 collective-permute-done.3.b_ref
  97.8 0.0 copy-start.15
  97.8 0.0 collective-permute-done.4.c_ref
  97.8 0.0 copy-start.16
  97.9 0.0 collective-permute-done.5.d_ref
  97.9 0.0 copy-done.14
  97.9 0.6 copy-done.15
  98.5 0.0 copy-done.16
  98.5 0.0 copy-start.17
  98.5 0.6 copy-done.17
  99.1 1.7 %mlp_place.1 = bf16[128,1024]{1,0:T(8,128)(2,1)} custom-call(bf16[32,1024]{1,0:T(8,128)(2,1)} %copy-done.14, bf16[32,1024]{1,0:T(8,128)(2,1)} %copy-done.15, bf16[32,1024]{1,0:T(8,128)(2,1)} %copy-done.16, bf16[32,1024]{1,0:T(8,128)(2,1)} %copy-done.17), custom_call_target="tpu_custom_call" | custom-call | tf_op jit(solution)/shard_map/mlp_place/pallas_call | solution.py:423
  (1 shorter events, 0.0 us)
Async XLA Ops:
  0.6 1.0 copy-start.1
  1.6 0.9 copy-start.2
  2.5 0.7 copy-start.4
  3.3 0.7 copy-start.5
  4.0 0.7 copy-start.6
  4.6 0.7 copy-start.7
  64.7 0.9 copy-start
  65.5 0.7 copy-start.3
  66.3 1.1 %copy-start.8 = (bf16[20,128,256]{2,1,0:T(8,128)(2,1)}, bf16[20,128,256]{2,1,0:T(8,128)(2,1)S(1)}, u32[]{:S(2)}) copy-start(bf16[20,128,256]{2,1,0:T(8,128)(2,1)S(1)} %get-tuple-element.26.du_ref) | copy-start | bytes 3932164
  67.3 0.7 copy-start.9
  68.0 0.6 copy-start.10
  68.6 0.6 copy-start.12
  69.2 0.6 copy-start.13
  69.8 4.1 %copy-start.11 = (f32[1,1024]{1,0:T(1,128)}, f32[1,1024]{1,0:T(1,128)S(1)}, u32[]{:S(2)}) copy-start(f32[1,1024]{1,0:T(1,128)S(1)} %get-tuple-element.29.db2_in) | copy-start | bytes 12292
  69.8 14.5 %collective-permute-start = (bf16[32,1024]{1,0:T(8,128)(2,1)S(1)}, bf16[32,1024]{1,0:T(8,128)(2,1)S(1)}, u32[]{:S(2)}, u32[]{:S(2)}) collective-permute-start(bf16[32,1024]{1,0:T(8,128)(2,1)S(1)} %get-tuple-element.34), channel_id=1, source_target_pairs={{0,4},{4,8},{8,12},{12,0},{1,5},{5,9},{9,13},{13,1},{2,6},{6,10},{... | collective-permute-start | bytes 196616 | tf_op jit(solution)/shard_map/ppermute | solution.py:398
  70.5 13.8 %collective-permute-start.1 = (bf16[32,1024]{1,0:T(8,128)(2,1)S(1)}, bf16[32,1024]{1,0:T(8,128)(2,1)S(1)}, u32[]{:S(2)}, u32[]{:S(2)}) collective-permute-start(bf16[32,1024]{1,0:T(8,128)(2,1)S(1)} %get-tuple-element.35), channel_id=1, source_target_pairs={{0,8},{4,12},{8,0},{12,4},{1,9},{5,13},{9,1},{13,5},{2,10},{6,14},... | collective-permute-start | bytes 196616 | tf_op jit(solution)/shard_map/ppermute | solution.py:398
  72.8 11.6 %collective-permute-start.2 = (bf16[32,1024]{1,0:T(8,128)(2,1)S(1)}, bf16[32,1024]{1,0:T(8,128)(2,1)S(1)}, u32[]{:S(2)}, u32[]{:S(2)}) collective-permute-start(bf16[32,1024]{1,0:T(8,128)(2,1)S(1)} %get-tuple-element.36), channel_id=1, source_target_pairs={{0,12},{4,0},{8,4},{12,8},{1,13},{5,1},{9,5},{13,9},{2,14},{6,2},{... | collective-permute-start | bytes 196616 | tf_op jit(solution)/shard_map/ppermute | solution.py:398
  84.4 13.5 %copy-start.14 = (bf16[32,1024]{1,0:T(8,128)(2,1)}, bf16[32,1024]{1,0:T(8,128)(2,1)S(1)}, u32[]{:S(2)}) copy-start(bf16[32,1024]{1,0:T(8,128)(2,1)S(1)} %add_convert_fusion.a_ref) | copy-start | bytes 196612
  84.4 13.4 %collective-permute-start.3 = (bf16[32,1024]{1,0:T(8,128)(2,1)S(1)}, bf16[32,1024]{1,0:T(8,128)(2,1)S(1)}, u32[]{:S(2)}, u32[]{:S(2)}) collective-permute-start(bf16[32,1024]{1,0:T(8,128)(2,1)S(1)} %add_convert_fusion.a_ref), channel_id=1, source_target_pairs={{0,4},{4,8},{8,12},{12,0},{1,5},{5,9},{9,13},{13,1},{2,6},{6,10},{... | collective-permute-start | bytes 196616 | tf_op jit(solution)/shard_map/ppermute | solution.py:398
  85.4 12.5 %collective-permute-start.4 = (bf16[32,1024]{1,0:T(8,128)(2,1)S(1)}, bf16[32,1024]{1,0:T(8,128)(2,1)S(1)}, u32[]{:S(2)}, u32[]{:S(2)}) collective-permute-start(bf16[32,1024]{1,0:T(8,128)(2,1)S(1)} %add_convert_fusion.a_ref), channel_id=1, source_target_pairs={{0,8},{4,12},{8,0},{12,4},{1,9},{5,13},{9,1},{13,5},{2,10},{6,14},... | collective-permute-start | bytes 196616 | tf_op jit(solution)/shard_map/ppermute | solution.py:398
  86.3 11.5 %collective-permute-start.5 = (bf16[32,1024]{1,0:T(8,128)(2,1)S(1)}, bf16[32,1024]{1,0:T(8,128)(2,1)S(1)}, u32[]{:S(2)}, u32[]{:S(2)}) collective-permute-start(bf16[32,1024]{1,0:T(8,128)(2,1)S(1)} %add_convert_fusion.a_ref), channel_id=1, source_target_pairs={{0,12},{4,0},{8,4},{12,8},{1,13},{5,1},{9,5},{13,9},{2,14},{6,2},{... | collective-permute-start | bytes 196616 | tf_op jit(solution)/shard_map/ppermute | solution.py:398
  97.8 0.6 copy-start.15
  97.8 0.6 copy-start.16
  98.5 0.6 copy-start.17

commit v2 on v1

v2 whole, which is shorter than its diff:
```python
import functools
import math

import jax
import jax.numpy as jnp
from jax import lax
from jax.experimental import pallas as pl
from jax.experimental.pallas import tpu as pltpu
from jax.sharding import PartitionSpec as P

PAIR = 128
ALPHA = math.sqrt(140.0)
LN_EPS = 1e-5
GELU_K = math.sqrt(2.0 / math.pi)
GELU_C = 0.044715
MESH = pl.DeviceIdType.MESH
F32 = jnp.float32
BF16 = jnp.bfloat16

GROUPS = 1
VMEM_LIMIT = 60 * 2**20
LOOKAHEAD = 3


def gelu_parts(z):
    t = jnp.tanh(GELU_K * (z + GELU_C * (z * z * z)))
    cdf = 0.5 * (1.0 + t)
    slope = cdf + z * (0.5 * (1.0 - t * t) * (GELU_K * (1.0 + (3.0 * GELU_C) * (z * z))))
    return z * cdf, slope


def dot_nt(a, b):
    return lax.dot_general(a, b, (((1,), (1,)), ((), ())), preferred_element_type=F32)


def dot_tn(a, b):
    return lax.dot_general(a, b, (((0,), (0,)), ((), ())), preferred_element_type=F32)


def main_kernel(
    x_hbm, w1_hbm, b1_hbm, w2_hbm, b2_hbm, gam_hbm, bet_hbm, dy_hbm,
    y_hbm, m_hbm, d_hbm, du_hbm, xg_hbm, db1_hbm, dsm_hbm,
    y_ref, m_ref, d_ref, du_ref, db1_ref, dsm_ref,
    x_ref, dy_ref, b1_ref, b2_ref, gam_ref, bet_ref,
    w1b, w2b, upart, uhalf, usend, uin, ubuf, mbuf, facc, zsend, zin, fsum, stat_in, stat_all, tmp, dr_buf,
    npart, nhalf, nsend, nin, nbuf, dxacc, xsend, xin, xown,
    wsem, isem, osem, chunk_s, chunk_r, full_s, full_r, zsem_s, zsem_r,
):
    n_ch = w1b.shape[0]
    tokens, hid = x_ref.shape
    hidden = 4 * hid
    tn = tokens // GROUPS
    rz = tn // 4
    cw = 8 * PAIR
    q = lax.axis_index('hd')
    z = lax.axis_index('ff')
    k = lax.rem(q, 2)
    y = lax.div(q, 2)
    pq = q + 1 - 2 * k
    yq = lax.rem(q + 2, 4)

    def remote(src, dst, ss, rs, **dev):
        return pltpu.make_async_remote_copy(src_ref=src, dst_ref=dst, send_sem=ss, recv_sem=rs, device_id=dev, device_id_type=MESH)

    w_copies = [pltpu.make_async_copy(w1_hbm.at[:, pl.ds(cw * c, cw)], w1b.at[c], wsem.at[c]) for c in range(n_ch)]
    w_copies += [pltpu.make_async_copy(w2_hbm.at[pl.ds(4 * PAIR * c, 4 * PAIR), :], w2b.at[c], wsem.at[n_ch + c]) for c in range(n_ch)]
    in_copies = [pltpu.make_async_copy(a, b, isem.at[i]) for i, (a, b) in enumerate(((x_hbm, x_ref), (b1_hbm, b1_ref), (dy_hbm, dy_ref), (b2_hbm, b2_ref), (gam_hbm, gam_ref), (bet_hbm, bet_ref)))]
    started = [0]
    landed = set()

    def need_weight(i):
        while started[0] < min(i + LOOKAHEAD, 2 * n_ch):
            w_copies[started[0]].start()
            started[0] += 1
        if i not in landed:
            landed.add(i)
            w_copies[i].wait()

    bar = pltpu.get_barrier_semaphore()
    for d in range(1, 4):
        pl.semaphore_signal(bar, inc=1, device_id={'ff': lax.rem(z + d, 4)}, device_id_type=MESH)
    for d in range(1, 4):
        pl.semaphore_signal(bar, inc=1, device_id={'hd': lax.rem(q + d, 4)}, device_id_type=MESH)
    in_copies[0].start()
    for i in range(LOOKAHEAD):
        w_copies[i].start()
    started[0] = LOOKAHEAD
    for cp in in_copies[1:]:
        cp.start()

    tmp[...] = jnp.zeros_like(tmp)
    waits = []
    outs = []

    def put(src, dst):
        cp = pltpu.make_async_copy(src, dst, osem.at[len(outs)])
        cp.start()
        outs.append(cp)

    seen = set()

    def once(name):
        new = name not in seen
        seen.add(name)
        return new

    def make_group(g):
        row0 = g * tn
        rows = pl.ds(row0, tn)

        def ch(kind, c):
            return chunk_s.at[g, kind, c], chunk_r.at[g, kind, c]

        u_d2d = [remote(upart.at[g, c, 1 - k], uhalf.at[g, c], *ch(0, c), hd=pq) for c in range(n_ch)]
        u_y = [remote(usend.at[g, c], uin.at[g, c], *ch(1, c), hd=yq) for c in range(n_ch)]
        m_p = [remote(mbuf.at[g, c, q], mbuf.at[g, c, q], *ch(2, c), hd=pq) for c in range(n_ch)]
        m_y = [remote(mbuf.at[g, c, q], mbuf.at[g, c, q], *ch(3, c), hd=yq) for c in range(n_ch)]
        m_f = [remote(mbuf.at[g, c, yq], mbuf.at[g, c, yq], *ch(4, c), hd=pq) for c in range(n_ch)]
        n_d2d = [remote(npart.at[g, c, 1 - k], nhalf.at[g, c], *ch(5, c), hd=pq) for c in range(n_ch)]
        n_y = [remote(nsend.at[g, c], nin.at[g, c], *ch(6, c), hd=yq) for c in range(n_ch)]
        n_p = [remote(nbuf.at[g, c, q], nbuf.at[g, c, q], *ch(7, c), hd=pq) for c in range(n_ch)]
        n_yy = [remote(nbuf.at[g, c, q], nbuf.at[g, c, q], *ch(8, c), hd=yq) for c in range(n_ch)]
        n_f = [remote(nbuf.at[g, c, yq], nbuf.at[g, c, yq], *ch(9, c), hd=pq) for c in range(n_ch)]
        u_p = remote(ubuf.at[g, q], ubuf.at[g, q], full_s.at[g, 0], full_r.at[g, 0], hd=pq)
        u_yy = remote(ubuf.at[g, q], ubuf.at[g, q], full_s.at[g, 1], full_r.at[g, 1], hd=yq)
        u_f = remote(ubuf.at[g, yq], ubuf.at[g, yq], full_s.at[g, 2], full_r.at[g, 2], hd=pq)

        def zc(kind, src, dst):
            return [remote(src(d), dst(d), zsem_s.at[g, kind, d - 1], zsem_r.at[g, kind, d - 1], ff=lax.rem(z + d, 4)) for d in range(1, 4)]

        z_rs = zc(0, lambda d: zsend.at[g, lax.rem(z + d, 4)], lambda d: zin.at[g, d - 1])
        z_ag = zc(1, lambda d: fsum.at[g, z], lambda d: fsum.at[g, z])
        z_st = zc(2, lambda d: stat_all.at[g, z], lambda d: stat_all.at[g, z])
        x_rs = zc(3, lambda d: xsend.at[g, lax.rem(z + d, 4)], lambda d: xin.at[g, d - 1])
        st = [remote(stat_in.at[g, q], stat_in.at[g, q], zsem_s.at[g, 5, d - 1], zsem_r.at[g, 5, d - 1], hd=lax.rem(q + d, 4)) for d in range(1, 4)]
        waits.extend(u_d2d + u_y + m_p + m_y + m_f + n_d2d + n_y + n_p + n_yy + n_f + [u_p, u_yy, u_f] + z_rs + z_ag + z_st + x_rs + st)

        def s1(c):
            if once('x'):
                in_copies[0].wait()
            need_weight(c)
            for j in range(4):
                o = jnp.dot(x_ref[rows, :], w1b[c, :, 2 * PAIR * j:2 * PAIR * (j + 1)], preferred_element_type=F32)
                upart[g, c, j % 2, j // 2] = o.astype(BF16)

        def sd(c):
            u_d2d[c].start()

        def s2(c):
            u_d2d[c].wait_recv()
            usend[g, c] = (upart[g, c, k, 1 - y].astype(F32) + uhalf[g, c, 1 - y].astype(F32)).astype(BF16)
            u_y[c].start()

        def s3(c):
            if once('in'):
                for cp in in_copies[1:]:
                    cp.wait()
            u_y[c].wait_recv()
            u = upart[g, c, k, y].astype(F32) + uhalf[g, c, y].astype(F32) + uin[g, c].astype(F32)
            u = (u + b1_ref[4 * c + q]).astype(BF16)
            ubuf[g, q, c] = u
            u = u.astype(F32)
            gl, _ = gelu_parts(u[:, PAIR:])
            mbuf[g, c, q] = (u[:, :PAIR] * gl).astype(BF16)
            m_y[c].start()
            m_p[c].start()

        def s4(c):
            m_y[c].wait_recv()
            m_f[c].start()

        def s5(c):
            need_weight(n_ch + c)
            m_p[c].wait_recv()
            m_f[c].wait_recv()
            blocks = [mbuf[g, c, j] for j in range(4)]
            for j in range(4):
                m_ref[4 * c + j, rows, :] = blocks[j]
            m = jnp.concatenate(blocks, axis=1)
            for n in range(0, hid, 256):
                o = jnp.dot(m, w2b[c, :, n:n + 256], preferred_element_type=F32)
                if c:
                    facc[g, :, n:n + 256] += o
                else:
                    facc[g, :, n:n + 256] = o

        def ug():
            u_yy.start()
            u_p.start()

        def uf():
            u_yy.wait_recv()
            u_f.start()

        def ud():
            u_p.wait_recv()
            u_f.wait_recv()

        def z1():
            for b in range(4):
                zsend[g, b] = facc[g, b * rz:(b + 1) * rz, :].astype(BF16)
            for d in (2, 1, 3):
                z_rs[d - 1].start()

        def z2():
            off = pl.multiple_of(z * rz, rz)
            f = facc[g, pl.ds(off, rz), :]
            for d in (1, 3, 2):
                z_rs[d - 1].wait_recv()
                f = f + zin[g, d - 1].astype(F32)
            f = f.astype(BF16)
            fsum[g, z] = f
            for d in (2, 1, 3):
                z_ag[d - 1].start()
            xoff = pl.multiple_of(row0 + z * rz, rz)
            r = ALPHA * x_ref[pl.ds(xoff, rz), :].astype(F32) + f.astype(F32) + b2_ref[...]
            gd = dy_ref[pl.ds(xoff, rz), :].astype(F32) * gam_ref[...]
            mean = jnp.sum(r, axis=1, keepdims=True) * (1.0 / hid)
            cen = r - mean
            m2 = jnp.sum(cen * cen, axis=1, keepdims=True)
            sg = jnp.sum(gd, axis=1, keepdims=True)
            sgr = jnp.sum(gd * cen, axis=1, keepdims=True)
            lane = lax.broadcasted_iota(jnp.int32, (rz, 128), 1)
            vals = jnp.where(lane == 0, mean, jnp.where(lane == 1, m2, jnp.where(lane == 2, sg, jnp.where(lane == 3, sgr, 0.0))))
            stat_in[g, q] = vals
            for s in st:
                s.start()

        def zb():
            for s in st:
                s.wait_recv()
            per = [stat_in[g, h] for h in range(4)]
            mu = sum(p[:, 0:1] for p in per) * 0.25
            m2 = sum(p[:, 1:2] + float(hid) * (p[:, 0:1] - mu) * (p[:, 0:1] - mu) for p in per)
            rho = lax.rsqrt(m2 * (1.0 / hidden) + LN_EPS)
            mg = sum(p[:, 2:3] for p in per) * (1.0 / hidden)
            mgr = rho * sum(p[:, 3:4] + (p[:, 0:1] - mu) * p[:, 2:3] for p in per) * (1.0 / hidden)
            lane = lax.broadcasted_iota(jnp.int32, (rz, 128), 1)
            tmp[:rz, :] = jnp.where(lane == 0, mu, jnp.where(lane == 1, rho, jnp.where(lane == 2, mg, jnp.where(lane == 3, mgr, 0.0))))
            stat_all[g, z] = tmp[...].T[:8, :]
            for s in z_st:
                s.start()

        def z3():
            for s in z_ag + z_st:
                s.wait_recv()
            for b in range(4):
                tmp[8 * b:8 * (b + 1), :] = stat_all[g, b]
            cols = tmp[...].T
            for b in range(4):
                rr = pl.ds(row0 + b * rz, rz)
                c4 = cols[:rz, 8 * b:8 * b + 4]
                r = ALPHA * x_ref[rr, :].astype(F32) + fsum[g, b].astype(F32) + b2_ref[...]
                dy = dy_ref[rr, :].astype(F32)
                rhat = (r - c4[:, 0:1]) * c4[:, 1:2]
                y_ref[rr, :] = (gam_ref[...] * rhat + bet_ref[...]).astype(BF16)
                dr = c4[:, 1:2] * (dy * gam_ref[...] - c4[:, 2:3] - rhat * c4[:, 3:4])
                dr_buf[rr, :] = dr
                d_ref[rr, :] = dr.astype(BF16)
                sums = (jnp.sum(dr, axis=0, keepdims=True), jnp.sum(dy * rhat, axis=0, keepdims=True), jnp.sum(dy, axis=0, keepdims=True))
                for i, s in enumerate(sums):
                    if g == 0 and b == 0:
                        dsm_ref[i] = s
                    else:
                        dsm_ref[i] += s

        def t1(c):
            for h in range(2):
                o = dot_nt(d_ref[rows, :], w2b[c, 256 * h:256 * (h + 1), :]).astype(BF16)
                npart[g, c, 0, h] = o[:, :PAIR]
                npart[g, c, 1, h] = o[:, PAIR:]
            n_d2d[c].start()
            if c == n_ch - 1:
                put(y_ref.at[rows, :], y_hbm.at[rows, :])
                put(d_ref.at[rows, :], d_hbm.at[rows, :])

        def t2(c):
            n_d2d[c].wait_recv()
            nsend[g, c] = (npart[g, c, k, 1 - y].astype(F32) + nhalf[g, c, 1 - y].astype(F32)).astype(BF16)
            n_y[c].start()

        def t3(c):
            n_y[c].wait_recv()
            nbuf[g, c, q] = (npart[g, c, k, y].astype(F32) + nhalf[g, c, y].astype(F32) + nin[g, c].astype(F32)).astype(BF16)
            n_yy[c].start()
            n_p[c].start()

        def t4(c):
            n_yy[c].wait_recv()
            n_f[c].start()

        def t5(c):
            n_p[c].wait_recv()
            n_f[c].wait_recv()
            parts = []
            for j in range(4):
                dm = nbuf[g, c, j].astype(F32)
                u = ubuf[g, j, c].astype(F32)
                gl, slope = gelu_parts(u[:, PAIR:])
                dv = dm * gl
                dg = dm * u[:, :PAIR] * slope
                duf = jnp.concatenate([dv, dg], axis=1)
                s = jnp.sum(duf, axis=0, keepdims=True)
                if g == 0:
                    db1_ref[4 * c + j] = s
                else:
                    db1_ref[4 * c + j] += s
                du = duf.astype(BF16)
                du_ref[4 * c + j, rows, :] = du
                parts.append(du)
            du = jnp.concatenate(parts, axis=1)
            for n in range(0, hid, 256):
                o = dot_nt(du, w1b[c, n:n + 256, :])
                if c:
                    dxacc[rows, n:n + 256] += o
                else:
                    dxacc[rows, n:n + 256] = o
            put(du_ref.at[pl.ds(4 * c, 4), rows, :], du_hbm.at[pl.ds(4 * c, 4), rows, :])

        def x1():
            put(db1_ref, db1_hbm)
            put(dsm_ref, dsm_hbm)
            for b in range(4):
                xsend[g, b] = dxacc[row0 + b * rz:row0 + (b + 1) * rz, :].astype(BF16)
            for d in (2, 1, 3):
                x_rs[d - 1].start()

        def x2():
            off = pl.multiple_of(row0 + z * rz, rz)
            t = ALPHA * dr_buf[pl.ds(off, rz), :] + dxacc[pl.ds(off, rz), :]
            for d in (1, 3, 2):
                x_rs[d - 1].wait_recv()
                t = t + xin[g, d - 1].astype(F32)
            t = t.astype(BF16)
            xown[g] = t
            for b in range(4):
                put(xown.at[g], xg_hbm.at[b])

        return dict(s1=s1, sd=sd, s2=s2, s3=s3, s4=s4, s5=s5, ug=ug, uf=uf, ud=ud, z1=z1, z2=z2, zb=zb, z3=z3, t1=t1, t2=t2, t3=t3, t4=t4, t5=t5, x1=x1, x2=x2)

    groups = {n: make_group(i) for i, n in enumerate('AB'[:GROUPS])}
    for name in order(n_ch):
        with jax.named_scope(name):
            if name == 'barrier':
                pl.semaphore_wait(bar, 6)
            elif name == 'mout':
                put(m_ref, m_hbm)
            else:
                groups[name[2]][name[:2]](*map(int, name[3:]))
    with jax.named_scope('finish'):
        for w in waits:
            w.wait_send()
        for w in outs:
            w.wait()


def order(n):
    def seq(name):
        return [f'{name}A{c}' for c in range(n)]

    o = ['s1A0', 'barrier', 'sdA0']
    for c in range(1, n):
        o += [f's1A{c}', f'sdA{c}', f's2A{c - 1}']
    o += [f's2A{n - 1}'] + seq('s3') + ['s4A0', 's4A1']
    for c in range(n):
        o += [f's5A{c}'] + ([f's4A{c + 2}'] if c + 2 < n else [])
    o += ['z1A', 'ugA', 'mout', 'z2A', 'zbA', 'ufA', 'z3A', 't1A0']
    for c in range(1, n):
        o += [f't1A{c}', f't2A{c - 1}']
    o += [f't2A{n - 1}', 'udA'] + seq('t3') + ['t4A0', 't4A1']
    for c in range(n):
        o += [f't5A{c}'] + ([f't4A{c + 2}'] if c + 2 < n else [])
    return o + ['x1A', 'x2A']


def grad_kernel(
    m_hbm, d_hbm, x_hbm, du_hbm, y_in, db1_in, dsm_in,
    dw1_hbm, dw2_hbm, y_hbm, db1_hbm, db2_hbm, dgam_hbm, dbet_hbm,
    m_ref, d_ref, x_ref, du_ref, y_ref, db1_ref, dsm_ref, dw1b, dw2b, isem, sem,
):
    n_blocks = m_ref.shape[0]
    hid = x_ref.shape[1]
    n_ch = n_blocks // 4
    copies = []
    loads = []

    def get(src, dst):
        cp = pltpu.make_async_copy(src, dst, isem.at[len(loads)])
        cp.start()
        loads.append(cp)

    def put(src, dst):
        cp = pltpu.make_async_copy(src, dst, sem.at[len(copies)])
        cp.start()
        copies.append(cp)

    get(d_hbm, d_ref)
    for c in range(n_ch):
        get(m_hbm.at[pl.ds(4 * c, 4)], m_ref.at[pl.ds(4 * c, 4)])
    loads[0].wait()
    for c in range(n_ch):
        loads[1 + c].wait()
        for i in range(4 * c, 4 * c + 4, 2):
            for j in range(2):
                dw2b[PAIR * (i + j):PAIR * (i + j + 1), :] = dot_tn(m_ref[i + j], d_ref[...])
            put(dw2b.at[pl.ds(PAIR * i, 2 * PAIR), :], dw2_hbm.at[pl.ds(PAIR * i, 2 * PAIR), :])
        if c == 0:
            for a, b in ((x_hbm, x_ref), (du_hbm, du_ref), (y_in, y_ref), (db1_in, db1_ref), (dsm_in, dsm_ref)):
                get(a, b)
    loads[1 + n_ch].wait()
    loads[2 + n_ch].wait()
    for i in range(0, hid, PAIR):
        for j in range(n_blocks):
            dw1b[i:i + PAIR, 2 * PAIR * j:2 * PAIR * (j + 1)] = dot_tn(x_ref[:, i:i + PAIR], du_ref[j])
        put(dw1b.at[pl.ds(i, PAIR), :], dw1_hbm.at[pl.ds(i, PAIR), :])
    for cp in loads[3 + n_ch:]:
        cp.wait()
    for a, b in ((y_ref, y_hbm), (db1_ref, db1_hbm), (dsm_ref.at[0], db2_hbm), (dsm_ref.at[1], dgam_hbm), (dsm_ref.at[2], dbet_hbm)):
        put(a, b)
    for cp in copies:
        cp.wait()


def solution(mesh):
    data_spec = P('dp', 'hd')
    hid_spec = P('hd')
    in_specs = (data_spec, P('hd', 'ff'), P('ff'), P('ff', 'hd'), hid_spec, hid_spec, hid_spec, data_spec)
    out_specs = (data_spec, data_spec, P(('dp', 'hd'), 'ff'), P(('dp', 'ff'), 'hd'), P(('dp', 'ff')), P(('dp', 'hd')), P(('dp', 'hd')), P(('dp', 'hd')))
    hbm = pl.BlockSpec(memory_space=pltpu.HBM)
    S = jax.ShapeDtypeStruct

    def device_step(x_loc, w_up, b_up, w_down, b_down, ln_gain, ln_bias, dy_loc):
        tokens, hid = x_loc.shape
        n_blocks = w_up.shape[1] // (2 * PAIR)
        n_ch = n_blocks // 4
        tn = tokens // GROUPS
        g = GROUPS
        rz = tn // 4
        V = pltpu.VMEM
        dma = pltpu.SemaphoreType.DMA
        outs = pl.pallas_call(
            main_kernel,
            out_shape=(
                S((tokens, hid), BF16), S((n_blocks, tokens, PAIR), BF16), S((tokens, hid), BF16), S((n_blocks, tokens, 2 * PAIR), BF16),
                S((4, rz, hid), BF16), S((n_blocks, 1, 2 * PAIR), F32), S((3, 1, hid), F32),
            ),
            in_specs=[hbm] * 8,
            out_specs=[hbm] * 7,
            scratch_shapes=[
                V((tokens, hid), BF16), V((n_blocks, tokens, PAIR), BF16), V((tokens, hid), BF16), V((n_blocks, tokens, 2 * PAIR), BF16),
                V((n_blocks, 1, 2 * PAIR), F32), V((3, 1, hid), F32),
                V((tokens, hid), BF16), V((tokens, hid), BF16), V((n_blocks, 1, 2 * PAIR), F32), V((1, hid), F32), V((1, hid), F32), V((1, hid), F32),
                V((n_ch, hid, 8 * PAIR), BF16), V((n_ch, 4 * PAIR, hid), BF16),
                V((g, n_ch, 2, 2, tn, 2 * PAIR), BF16), V((g, n_ch, 2, tn, 2 * PAIR), BF16), V((g, n_ch, tn, 2 * PAIR), BF16), V((g, n_ch, tn, 2 * PAIR), BF16),
                V((g, 4, n_ch, tn, 2 * PAIR), BF16), V((g, n_ch, 4, tn, PAIR), BF16),
                V((g, tn, hid), F32), V((g, 4, rz, hid), BF16), V((g, 3, rz, hid), BF16), V((g, 4, rz, hid), BF16),
                V((g, 4, rz, 128), F32), V((g, 4, 8, 128), F32), V((128, 128), F32), V((tokens, hid), F32),
                V((g, n_ch, 2, 2, tn, PAIR), BF16), V((g, n_ch, 2, tn, PAIR), BF16), V((g, n_ch, tn, PAIR), BF16), V((g, n_ch, tn, PAIR), BF16),
                V((g, n_ch, 4, tn, PAIR), BF16), V((tokens, hid), F32),
                V((g, 4, rz, hid), BF16), V((g, 3, rz, hid), BF16), V((g, rz, hid), BF16),
                dma((2 * n_ch,)), dma((6,)), dma(((2 + n_ch) * g + 7,)), dma((g, 10, n_ch)), dma((g, 10, n_ch)), dma((g, 3)), dma((g, 3)), dma((g, 6, 3)), dma((g, 6, 3)),
            ],
            compiler_params=pltpu.CompilerParams(collective_id=0, has_side_effects=True, vmem_limit_bytes=VMEM_LIMIT),
            name='mlp_main',
        )(x_loc, w_up, b_up.reshape(n_blocks, 1, 2 * PAIR), w_down, b_down.reshape(1, hid), ln_gain.reshape(1, hid), ln_bias.reshape(1, hid), dy_loc)
        y_a, m_a, d_a, du_a, xg, db1, dsm = outs
        dx = lax.all_to_all(xg, 'ff', 0, 0)
        vec = S((1, hid), F32)
        dw_up, dw_down, y_o, db1_o, db2_o, dg_o, dbt_o = pl.pallas_call(
            grad_kernel,
            out_shape=(S((hid, n_blocks * 2 * PAIR), F32), S((n_blocks * PAIR, hid), F32), S(y_a.shape, BF16), S(db1.shape, F32), vec, vec, vec),
            in_specs=[hbm] * 7,
            out_specs=[hbm] * 7,
            scratch_shapes=[
                V((n_blocks, tokens, PAIR), BF16), V((tokens, hid), BF16), V((tokens, hid), BF16), V((n_blocks, tokens, 2 * PAIR), BF16),
                V((tokens, hid), BF16), V((n_blocks, 1, 2 * PAIR), F32), V((3, 1, hid), F32),
                V((hid, n_blocks * 2 * PAIR), F32), V((n_blocks * PAIR, hid), F32), dma((6 + n_ch,)), dma((n_blocks // 2 + hid // PAIR + 5,)),
            ],
            compiler_params=pltpu.CompilerParams(vmem_limit_bytes=VMEM_LIMIT),
            cost_estimate=pl.CostEstimate(flops=10**10, bytes_accessed=10**7, transcendentals=0),
            name='mlp_grads',
        )(m_a, d_a, x_loc, du_a, y_a, db1, dsm)
        return (y_o, dx.reshape(tokens, hid), dw_up, dw_down, db1_o.reshape(-1), db2_o.reshape(-1), dg_o.reshape(-1), dbt_o.reshape(-1))

    return jax.shard_map(device_step, mesh=mesh, in_specs=in_specs, out_specs=out_specs, check_vma=False)
```

time: 102 us -> 75 us (0.74); the launches traced: 101 us -> 74.8 us
  Pallas kernels: 80.1 us -> 69.5 us
  local copies, waits for them, and re-layouts: 11 us -> 0.71 us
  starting transfers between devices: 8.83 us -> 3.9 us
    unnamed x36 -> x1, local copies, waits for them, and re-layouts: 11 us -> 0.71 us
    pallas_call x3 -> x1, Pallas kernels: 20.8 us -> 11.9 us  [device_step(): pl.pallas_call(grad_kernel, out_shape=(S((hid, n_blocks * 2 * PAIR), F32)...]
    ppermute x6 -> x0, starting transfers between devices: 8.83 us -> none  [shift(): return lax.ppermute(v, 'ff', [(i, (i + d) % n_ff) for i in range(n_ff)])]
    all_to_all x0 -> x1, starting transfers between devices: none -> 3.9 us  [device_step(): dx = lax.all_to_all(xg, 'ff', 0, 0)]
    pallas_call x1, Pallas kernels: 59.3 us -> 57.6 us  [device_step(): pl.pallas_call(main_kernel, out_shape=(S((tokens, hid), BF16), S((n_block...]
  transfers between devices with their start and end apart: 6 -> 1, of which waited for: 0 -> 0; matrix products, arithmetic and copies ran while one was open for 0% -> 0% of each run, Pallas kernels for 19% -> 16%
where the time goes in v2:
time: 75 us; the launch traced here: 74.8 us
  Pallas kernels  69.5 us (93%)
  starting transfers between devices  3.9 us (5%)
    pallas_call x1, Pallas kernels, device_step(): pl.pallas_call(main_kernel, out_shape=(S((tokens, hid), BF16), S((n_block...  57.6 us
    pallas_call x1, Pallas kernels, device_step(): pl.pallas_call(grad_kernel, out_shape=(S((hid, n_blocks * 2 * PAIR), F32)...  11.9 us
    all_to_all x1, starting transfers between devices, device_step(): dx = lax.all_to_all(xg, 'ff', 0, 0)  3.9 us
  transfers between devices with their start and end apart: 1, of which 0 were waited for; matrix products, arithmetic and copies ran while one was open for 0% of the time, Pallas kernels for 16%

profile of v2, /device:TPU:0, one launch (start us, length us, event | category | flops | bytes accessed | tf_op | source)
XLA Modules:
  0.0 74.8 jit_solution(12570326954785928648)
XLA Ops:
  0.6 57.6 %mlp_main.1 = (bf16[128,1024]{1,0:T(8,128)(2,1)}, bf16[20,128,128]{2,1,0:T(8,128)(2,1)}, bf16[128,1024]{1,0:T(8,128)(2,1)}, bf16[20,128,256]{2,1,0:T(8,128)(2,1)...) custom-call(bf16[128,1024]{1,0:T(8,128)(2,1)} %x_hbm.3, bf16[1024,5120]{1,0:T(8,128)(2,1)} %w1_hbm.1, ...), custom_call_target="tpu_custom_call" | custom-call | tf_op jit(solution)/shard_map/mlp_main/pallas_call | solution.py:441
  58.3 3.9 %all-to-all-start = ((bf16[4,32,1024]{2,1,0:T(8,128)(2,1)}), bf16[4,32,1024]{2,1,0:T(8,128)(2,1)S(1)}, u32[]{:S(2)}, u32[]{:S(2)}) async-start(bf16[4,32,1024]{2,1,0:T(8,128)(2,1)} %get-tuple-element.29), calls=%async_computation | async-start | bytes 524288 | tf_op jit(solution)/shard_map/all_to_all | solution.py:467
  62.2 11.9 %mlp_grads.1 = (f32[1024,5120]{1,0:T(8,128)}, f32[2560,1024]{1,0:T(8,128)}, bf16[128,1024]{1,0:T(8,128)(2,1)}, f32[20,1,256]{2,1,0:T(1,128)}, f32[1,1024]{1,0:T(...) custom-call(bf16[20,128,128]{2,1,0:T(8,128)(2,1)} %get-tuple-element.22.m_hbm, bf16[128,1024]{1,0:T(8,128)(2,1)} %get-tuple-element.23.d_hbm, ...), custom_call_target="tpu_custom_call" | custom-call | flops 10000000000 | bytes 10000000 | tf_op jit(solution)/shard_map/mlp_grads/pallas_call | solution.py:469
  74.1 0.0 all-to-all-done
  74.1 0.7 copy.17
Async XLA Ops:
  58.3 15.8 %all-to-all-start = ((bf16[4,32,1024]{2,1,0:T(8,128)(2,1)}), bf16[4,32,1024]{2,1,0:T(8,128)(2,1)S(1)}, u32[]{:S(2)}, u32[]{:S(2)}) async-start(bf16[4,32,1024]{2,1,0:T(8,128)(2,1)} %get-tuple-element.29), calls=%async_computation | async-start | bytes 524288 | tf_op jit(solution)/shard_map/all_to_all | solution.py:467

commit v3 on v2

--- a/solution.py
+++ b/solution.py
@@ -58,6 +58,8 @@
     y = lax.div(q, 2)
     pq = q + 1 - 2 * k
     yq = lax.rem(q + 2, 4)
+    dq = lax.rem(pq + 2, 4)
+    last = n_ch - 1
 
     def remote(src, dst, ss, rs, **dev):
         return pltpu.make_async_remote_copy(src_ref=src, dst_ref=dst, send_sem=ss, recv_sem=rs, device_id=dev, device_id_type=MESH)
@@ -115,12 +117,14 @@
         u_y = [remote(usend.at[g, c], uin.at[g, c], *ch(1, c), hd=yq) for c in range(n_ch)]
         m_p = [remote(mbuf.at[g, c, q], mbuf.at[g, c, q], *ch(2, c), hd=pq) for c in range(n_ch)]
         m_y = [remote(mbuf.at[g, c, q], mbuf.at[g, c, q], *ch(3, c), hd=yq) for c in range(n_ch)]
-        m_f = [remote(mbuf.at[g, c, yq], mbuf.at[g, c, yq], *ch(4, c), hd=pq) for c in range(n_ch)]
+        m_f = [remote(mbuf.at[g, c, yq], mbuf.at[g, c, yq], *ch(4, c), hd=pq) for c in range(last)]
+        m_f.append(remote(mbuf.at[g, last, q], mbuf.at[g, last, q], *ch(4, last), hd=dq))
         n_d2d = [remote(npart.at[g, c, 1 - k], nhalf.at[g, c], *ch(5, c), hd=pq) for c in range(n_ch)]
         n_y = [remote(nsend.at[g, c], nin.at[g, c], *ch(6, c), hd=yq) for c in range(n_ch)]
         n_p = [remote(nbuf.at[g, c, q], nbuf.at[g, c, q], *ch(7, c), hd=pq) for c in range(n_ch)]
         n_yy = [remote(nbuf.at[g, c, q], nbuf.at[g, c, q], *ch(8, c), hd=yq) for c in range(n_ch)]
-        n_f = [remote(nbuf.at[g, c, yq], nbuf.at[g, c, yq], *ch(9, c), hd=pq) for c in range(n_ch)]
+        n_f = [remote(nbuf.at[g, c, yq], nbuf.at[g, c, yq], *ch(9, c), hd=pq) for c in range(last)]
+        n_f.append(remote(nbuf.at[g, last, q], nbuf.at[g, last, q], *ch(9, last), hd=dq))
         u_p = remote(ubuf.at[g, q], ubuf.at[g, q], full_s.at[g, 0], full_r.at[g, 0], hd=pq)
         u_yy = remote(ubuf.at[g, q], ubuf.at[g, q], full_s.at[g, 1], full_r.at[g, 1], hd=yq)
         u_f = remote(ubuf.at[g, yq], ubuf.at[g, yq], full_s.at[g, 2], full_r.at[g, 2], hd=pq)
@@ -164,10 +168,13 @@
             mbuf[g, c, q] = (u[:, :PAIR] * gl).astype(BF16)
             m_y[c].start()
             m_p[c].start()
+            if c == last:
+                m_f[c].start()
 
         def s4(c):
             m_y[c].wait_recv()
-            m_f[c].start()
+            if c < last:
+                m_f[c].start()
 
         def s5(c):
             need_weight(n_ch + c)
@@ -241,28 +248,27 @@
             for s in z_st:
                 s.start()
 
-        def z3():
-            for s in z_ag + z_st:
-                s.wait_recv()
-            for b in range(4):
-                tmp[8 * b:8 * (b + 1), :] = stat_all[g, b]
-            cols = tmp[...].T
-            for b in range(4):
-                rr = pl.ds(row0 + b * rz, rz)
-                c4 = cols[:rz, 8 * b:8 * b + 4]
-                r = ALPHA * x_ref[rr, :].astype(F32) + fsum[g, b].astype(F32) + b2_ref[...]
-                dy = dy_ref[rr, :].astype(F32)
-                rhat = (r - c4[:, 0:1]) * c4[:, 1:2]
-                y_ref[rr, :] = (gam_ref[...] * rhat + bet_ref[...]).astype(BF16)
-                dr = c4[:, 1:2] * (dy * gam_ref[...] - c4[:, 2:3] - rhat * c4[:, 3:4])
-                dr_buf[rr, :] = dr
-                d_ref[rr, :] = dr.astype(BF16)
-                sums = (jnp.sum(dr, axis=0, keepdims=True), jnp.sum(dy * rhat, axis=0, keepdims=True), jnp.sum(dy, axis=0, keepdims=True))
-                for i, s in enumerate(sums):
-                    if g == 0 and b == 0:
-                        dsm_ref[i] = s
-                    else:
-                        dsm_ref[i] += s
+        def z3(d):
+            if d:
+                z_ag[d - 1].wait_recv()
+                z_st[d - 1].wait_recv()
+            src = lax.rem(z + 4 - d, 4)
+            tmp[:8, :] = stat_all[g, src]
+            c4 = tmp[...].T[:rz, :4]
+            rr = pl.ds(pl.multiple_of(row0 + src * rz, rz), rz)
+            r = ALPHA * x_ref[rr, :].astype(F32) + fsum[g, src].astype(F32) + b2_ref[...]
+            dy = dy_ref[rr, :].astype(F32)
+            rhat = (r - c4[:, 0:1]) * c4[:, 1:2]
+            y_ref[rr, :] = (gam_ref[...] * rhat + bet_ref[...]).astype(BF16)
+            dr = c4[:, 1:2] * (dy * gam_ref[...] - c4[:, 2:3] - rhat * c4[:, 3:4])
+            dr_buf[rr, :] = dr
+            d_ref[rr, :] = dr.astype(BF16)
+            sums = (jnp.sum(dr, axis=0, keepdims=True), jnp.sum(dy * rhat, axis=0, keepdims=True), jnp.sum(dy, axis=0, keepdims=True))
+            for i, s in enumerate(sums):
+                if g == 0 and d == 0:
+                    dsm_ref[i] = s
+                else:
+                    dsm_ref[i] += s
 
         def t1(c):
             for h in range(2):
@@ -284,10 +290,13 @@
             nbuf[g, c, q] = (npart[g, c, k, y].astype(F32) + nhalf[g, c, y].astype(F32) + nin[g, c].astype(F32)).astype(BF16)
             n_yy[c].start()
             n_p[c].start()
+            if c == last:
+                n_f[c].start()
 
         def t4(c):
             n_yy[c].wait_recv()
-            n_f[c].start()
+            if c < last:
+                n_f[c].start()
 
         def t5(c):
             n_p[c].wait_recv()
@@ -364,7 +373,7 @@
     o += [f's2A{n - 1}'] + seq('s3') + ['s4A0', 's4A1']
     for c in range(n):
         o += [f's5A{c}'] + ([f's4A{c + 2}'] if c + 2 < n else [])
-    o += ['z1A', 'ugA', 'mout', 'z2A', 'zbA', 'ufA', 'z3A', 't1A0']
+    o += ['z1A', 'ugA', 'mout', 'z2A', 'zbA', 'z3A0', 'ufA', 'z3A1', 'z3A3', 'z3A2', 't1A0']
     for c in range(1, n):
         o += [f't1A{c}', f't2A{c - 1}']
     o += [f't2A{n - 1}', 'udA'] + seq('t3') + ['t4A0', 't4A1']

time: 75 us -> 74.5 us (level)
  no operation moved by 1% of the time
where the time goes in v3:
time: 74.5 us; the launch traced here: 74.3 us
  Pallas kernels  69.3 us (93%)
  starting transfers between devices  3.6 us (5%)
    pallas_call x1, Pallas kernels, device_step(): pl.pallas_call(main_kernel, out_shape=(S((tokens, hid), BF16), S((n_block...  57.4 us
    pallas_call x1, Pallas kernels, device_step(): pl.pallas_call(grad_kernel, out_shape=(S((hid, n_blocks * 2 * PAIR), F32)...  11.9 us
    all_to_all x1, starting transfers between devices, device_step(): dx = lax.all_to_all(xg, 'ff', 0, 0)  3.6 us
  transfers between devices with their start and end apart: 1, of which 0 were waited for; matrix products, arithmetic and copies ran while one was open for 0% of the time, Pallas kernels for 16%

profile of v3, /device:TPU:0, one launch (start us, length us, event | category | flops | bytes accessed | tf_op | source)
XLA Modules:
  0.0 74.3 jit_solution(5417064645055844212)
XLA Ops:
  0.6 57.4 %mlp_main.1 = (bf16[128,1024]{1,0:T(8,128)(2,1)}, bf16[20,128,128]{2,1,0:T(8,128)(2,1)}, bf16[128,1024]{1,0:T(8,128)(2,1)}, bf16[20,128,256]{2,1,0:T(8,128)(2,1)...) custom-call(bf16[128,1024]{1,0:T(8,128)(2,1)} %x_hbm.3, bf16[1024,5120]{1,0:T(8,128)(2,1)} %w1_hbm.1, ...), custom_call_target="tpu_custom_call" | custom-call | tf_op jit(solution)/shard_map/mlp_main/pallas_call | solution.py:450
  58.1 3.6 %all-to-all-start = ((bf16[4,32,1024]{2,1,0:T(8,128)(2,1)}), bf16[4,32,1024]{2,1,0:T(8,128)(2,1)S(1)}, u32[]{:S(2)}, u32[]{:S(2)}) async-start(bf16[4,32,1024]{2,1,0:T(8,128)(2,1)} %get-tuple-element.29), calls=%async_computation | async-start | bytes 524288 | tf_op jit(solution)/shard_map/all_to_all | solution.py:476
  61.7 11.9 %mlp_grads.1 = (f32[1024,5120]{1,0:T(8,128)}, f32[2560,1024]{1,0:T(8,128)}, bf16[128,1024]{1,0:T(8,128)(2,1)}, f32[20,1,256]{2,1,0:T(1,128)}, f32[1,1024]{1,0:T(...) custom-call(bf16[20,128,128]{2,1,0:T(8,128)(2,1)} %get-tuple-element.22.m_hbm, bf16[128,1024]{1,0:T(8,128)(2,1)} %get-tuple-element.23.d_hbm, ...), custom_call_target="tpu_custom_call" | custom-call | flops 10000000000 | bytes 10000000 | tf_op jit(solution)/shard_map/mlp_grads/pallas_call | solution.py:478
  73.6 0.0 all-to-all-done
  73.6 0.7 copy.17
Async XLA Ops:
  58.1 15.5 %all-to-all-start = ((bf16[4,32,1024]{2,1,0:T(8,128)(2,1)}), bf16[4,32,1024]{2,1,0:T(8,128)(2,1)S(1)}, u32[]{:S(2)}, u32[]{:S(2)}) async-start(bf16[4,32,1024]{2,1,0:T(8,128)(2,1)} %get-tuple-element.29), calls=%async_computation | async-start | bytes 524288 | tf_op jit(solution)/shard_map/all_to_all | solution.py:476

commit v4 on v3

--- a/solution.py
+++ b/solution.py
@@ -59,6 +59,9 @@
     pq = q + 1 - 2 * k
     yq = lax.rem(q + 2, 4)
     dq = lax.rem(pq + 2, 4)
+    pair, place = lax.div(z, 2), lax.rem(z, 2)
+    inner = pair + place - 2 * pair * place
+    d_a, d_b = 3 - 2 * pair, 1 + 2 * pair
     last = n_ch - 1
 
     def remote(src, dst, ss, rs, **dev):
@@ -133,8 +136,14 @@
             return [remote(src(d), dst(d), zsem_s.at[g, kind, d - 1], zsem_r.at[g, kind, d - 1], ff=lax.rem(z + d, 4)) for d in range(1, 4)]
 
         z_rs = zc(0, lambda d: zsend.at[g, lax.rem(z + d, 4)], lambda d: zin.at[g, d - 1])
-        z_ag = zc(1, lambda d: fsum.at[g, z], lambda d: fsum.at[g, z])
+        def gather(d, block, dev):
+            return remote(fsum.at[g, block], fsum.at[g, block], zsem_s.at[g, 1, d - 1], zsem_r.at[g, 1, d - 1], ff=dev)
+
+        z_ag = [gather(d_a, z, lax.rem(z + d_a, 4)), gather(2, z + inner * (3 - 2 * z), (1 - inner) * lax.rem(z + 2, 4) + inner * (z + 1 - 2 * place)), gather(d_b, z, lax.rem(z + d_b, 4))]
+        z_sd = [remote(stat_all.at[g, z], stat_all.at[g, z], zsem_s.at[g, 2, d - 1], zsem_r.at[g, 2, d - 1], ff=lax.rem(z + d, 4)) for d in (d_a, 2, d_b)]
         z_st = zc(2, lambda d: stat_all.at[g, z], lambda d: stat_all.at[g, z])
+        z_out = [remote(zsend.at[g, lax.rem(z + d, 4)], zin.at[g, d - 1], zsem_s.at[g, 0, d - 1], zsem_r.at[g, 0, d - 1], ff=lax.rem(z + d, 4)) for d in (d_a, 2, d_b)]
+        x_out = [remote(xsend.at[g, lax.rem(z + d, 4)], xin.at[g, d - 1], zsem_s.at[g, 3, d - 1], zsem_r.at[g, 3, d - 1], ff=lax.rem(z + d, 4)) for d in (d_a, 2, d_b)]
         x_rs = zc(3, lambda d: xsend.at[g, lax.rem(z + d, 4)], lambda d: xin.at[g, d - 1])
         st = [remote(stat_in.at[g, q], stat_in.at[g, q], zsem_s.at[g, 5, d - 1], zsem_r.at[g, 5, d - 1], hd=lax.rem(q + d, 4)) for d in range(1, 4)]
         waits.extend(u_d2d + u_y + m_p + m_y + m_f + n_d2d + n_y + n_p + n_yy + n_f + [u_p, u_yy, u_f] + z_rs + z_ag + z_st + x_rs + st)
@@ -206,8 +215,8 @@
         def z1():
             for b in range(4):
                 zsend[g, b] = facc[g, b * rz:(b + 1) * rz, :].astype(BF16)
-            for d in (2, 1, 3):
-                z_rs[d - 1].start()
+            for cp in z_out:
+                cp.start()
 
         def z2():
             off = pl.multiple_of(z * rz, rz)
@@ -217,8 +226,9 @@
                 f = f + zin[g, d - 1].astype(F32)
             f = f.astype(BF16)
             fsum[g, z] = f
-            for d in (2, 1, 3):
-                z_ag[d - 1].start()
+            z_ag[2].start()
+            z_ag[0].start()
+            pl.when(inner == 0)(z_ag[1].start)
             xoff = pl.multiple_of(row0 + z * rz, rz)
             r = ALPHA * x_ref[pl.ds(xoff, rz), :].astype(F32) + f.astype(F32) + b2_ref[...]
             gd = dy_ref[pl.ds(xoff, rz), :].astype(F32) * gam_ref[...]
@@ -248,10 +258,14 @@
             for s in z_st:
                 s.start()
 
-        def z3(d):
-            if d:
-                z_ag[d - 1].wait_recv()
-                z_st[d - 1].wait_recv()
+        def z3(i):
+            d = (0, d_a, d_b, 2)[i]
+            if i:
+                e = (0, 2, 1)[i - 1]
+                z_ag[e].wait_recv()
+                if i == 1:
+                    pl.when(inner == 1)(z_ag[1].start)
+                z_sd[e].wait_recv()
             src = lax.rem(z + 4 - d, 4)
             tmp[:8, :] = stat_all[g, src]
             c4 = tmp[...].T[:rz, :4]
@@ -264,11 +278,11 @@
             dr_buf[rr, :] = dr
             d_ref[rr, :] = dr.astype(BF16)
             sums = (jnp.sum(dr, axis=0, keepdims=True), jnp.sum(dy * rhat, axis=0, keepdims=True), jnp.sum(dy, axis=0, keepdims=True))
-            for i, s in enumerate(sums):
-                if g == 0 and d == 0:
-                    dsm_ref[i] = s
+            for e, s in enumerate(sums):
+                if g == 0 and i == 0:
+                    dsm_ref[e] = s
                 else:
-                    dsm_ref[i] += s
+                    dsm_ref[e] += s
 
         def t1(c):
             for h in range(2):
@@ -331,8 +345,8 @@
             put(dsm_ref, dsm_hbm)
             for b in range(4):
                 xsend[g, b] = dxacc[row0 + b * rz:row0 + (b + 1) * rz, :].astype(BF16)
-            for d in (2, 1, 3):
-                x_rs[d - 1].start()
+            for cp in x_out:
+                cp.start()
 
         def x2():
             off = pl.multiple_of(row0 + z * rz, rz)
@@ -373,7 +387,7 @@
     o += [f's2A{n - 1}'] + seq('s3') + ['s4A0', 's4A1']
     for c in range(n):
         o += [f's5A{c}'] + ([f's4A{c + 2}'] if c + 2 < n else [])
-    o += ['z1A', 'ugA', 'mout', 'z2A', 'zbA', 'z3A0', 'ufA', 'z3A1', 'z3A3', 'z3A2', 't1A0']
+    o += ['z1A', 'ugA', 'mout', 'z2A', 'zbA', 'z3A0', 'ufA', 'z3A1', 'z3A2', 'z3A3', 't1A0']
     for c in range(1, n):
         o += [f't1A{c}', f't2A{c - 1}']
     o += [f't2A{n - 1}', 'udA'] + seq('t3') + ['t4A0', 't4A1']

time: 74.5 us -> 73.4 us (0.985)
  Pallas kernels: 69.3 us -> 68.2 us
    pallas_call x1, Pallas kernels: 57.4 us -> 56.3 us  [device_step(): pl.pallas_call(main_kernel, out_shape=(S((tokens, hid), BF16), S((n_block...]
where the time goes in v4:
time: 73.4 us; the launch traced here: 73.2 us
  Pallas kernels  68.2 us (93%)
  starting transfers between devices  3.6 us (5%)
    pallas_call x1, Pallas kernels, device_step(): pl.pallas_call(main_kernel, out_shape=(S((tokens, hid), BF16), S((n_block...  56.3 us
    pallas_call x1, Pallas kernels, device_step(): pl.pallas_call(grad_kernel, out_shape=(S((hid, n_blocks * 2 * PAIR), F32)...  11.9 us
    all_to_all x1, starting transfers between devices, device_step(): dx = lax.all_to_all(xg, 'ff', 0, 0)  3.6 us
  transfers between devices with their start and end apart: 1, of which 0 were waited for; matrix products, arithmetic and copies ran while one was open for 0% of the time, Pallas kernels for 16%

profile of v4, /device:TPU:0, one launch (start us, length us, event | category | flops | bytes accessed | tf_op | source)
XLA Modules:
  0.0 73.2 jit_solution(719870836256914056)
XLA Ops:
  0.6 56.3 %mlp_main.1 = (bf16[128,1024]{1,0:T(8,128)(2,1)}, bf16[20,128,128]{2,1,0:T(8,128)(2,1)}, bf16[128,1024]{1,0:T(8,128)(2,1)}, bf16[20,128,256]{2,1,0:T(8,128)(2,1)...) custom-call(bf16[128,1024]{1,0:T(8,128)(2,1)} %x_hbm.3, bf16[1024,5120]{1,0:T(8,128)(2,1)} %w1_hbm.1, ...), custom_call_target="tpu_custom_call" | custom-call | tf_op jit(solution)/shard_map/mlp_main/pallas_call | solution.py:464
  57.0 3.6 %all-to-all-start = ((bf16[4,32,1024]{2,1,0:T(8,128)(2,1)}), bf16[4,32,1024]{2,1,0:T(8,128)(2,1)S(1)}, u32[]{:S(2)}, u32[]{:S(2)}) async-start(bf16[4,32,1024]{2,1,0:T(8,128)(2,1)} %get-tuple-element.29), calls=%async_computation | async-start | bytes 524288 | tf_op jit(solution)/shard_map/all_to_all | solution.py:490
  60.6 11.9 %mlp_grads.1 = (f32[1024,5120]{1,0:T(8,128)}, f32[2560,1024]{1,0:T(8,128)}, bf16[128,1024]{1,0:T(8,128)(2,1)}, f32[20,1,256]{2,1,0:T(1,128)}, f32[1,1024]{1,0:T(...) custom-call(bf16[20,128,128]{2,1,0:T(8,128)(2,1)} %get-tuple-element.22.m_hbm, bf16[128,1024]{1,0:T(8,128)(2,1)} %get-tuple-element.23.d_hbm, ...), custom_call_target="tpu_custom_call" | custom-call | flops 10000000000 | bytes 10000000 | tf_op jit(solution)/shard_map/mlp_grads/pallas_call | solution.py:492
  72.5 0.0 all-to-all-done
  72.5 0.7 copy.17
Async XLA Ops:
  57.0 15.5 %all-to-all-start = ((bf16[4,32,1024]{2,1,0:T(8,128)(2,1)}), bf16[4,32,1024]{2,1,0:T(8,128)(2,1)S(1)}, u32[]{:S(2)}, u32[]{:S(2)}) async-start(bf16[4,32,1024]{2,1,0:T(8,128)(2,1)} %get-tuple-element.29), calls=%async_computation | async-start | bytes 524288 | tf_op jit(solution)/shard_map/all_to_all | solution.py:490
